TPU v7x, 32 devices: a whole 2x2x4 slice. The times are simulated.
32 devices in a mesh: cp: 8 (over z, y), fs: 4 (over x, core).
Axes of the slice: x: 2, y: 2, z: 4, core: 2. Of those that a mesh axis runs over, the one named last changes fastest.
Arguments:
- embeds: bfloat16 [4, 2048, 4096], P('fs', 'cp'), may hold values from -6 to 6
- queries: bfloat16 [4, 2048, 2048], P('fs', 'cp'), may hold values from -12 to 12
- key_heads: bfloat16 [4, 2048, 512], P('fs', 'cp'), may hold values from -4 to 4
- cotangent: bfloat16 [4, 2048, 2048], P('fs', 'cp'), may hold values from -6 to 6
- doc_start: int32 [4, 2048], P('fs', 'cp'), may hold values from 0 to 2047, as said below
- need_ids: int32 [4, 8, 5], P('fs', 'cp'), may hold values from -1 to 7, as said below
- y_weight: bfloat16 [4096, 512], P(('cp', 'fs')), may hold values from -0.09375 to 0.09375
- z_weight: float32 [4096, 512], P(('cp', 'fs')), may hold values from -0.09375 to 0.09375
- x_weight: float32 [4096, 512], P(('cp', 'fs')), may hold values from -0.09375 to 0.09375
- second_moment: float32 [4096, 512], P(('cp', 'fs')), may hold values from 1e-05 to 0.001
Outputs:
- z_next: float32 [4096, 512], P(('cp', 'fs'))
- x_next: float32 [4096, 512], P(('cp', 'fs'))
- moment_next: float32 [4096, 512], P(('cp', 'fs'))
- y_next: bfloat16 [4096, 512], P(('cp', 'fs'))
Inputs may be any that keep to these rules, and one draw needn't show every extreme that they name: `doc_start`: documents are contiguous and hold at most 1024 tokens, so a query block needs key-value blocks at most 4 blocks back; in every sequence some query block needs the block exactly 4 back. need_ids[f, b, j] is b - j when some query of block b is allowed a key of block b - j, else -1; need_ids[f, b, 0] is always b.
All inputs are finite; a program needn't handle non-finite values.
Results may differ from a plain program's by a relative error of at most 0.0027.
The roundings to bfloat16 on the way count: a program that leaves them out, or rounds other values in their place, can miss the bound.
Values may be sent and summed in bfloat16 or wider, within the bound.
A program may use at most 128 MiB of HBM per device.

v0:
```python
import math

import jax
import jax.numpy as jnp
from jax import lax
from jax.sharding import PartitionSpec as P

HEAD = 128
KV_HEADS = 4
WIN = 4
GROUP = 4


NORM_EPS = 0.01
MOMENT_DECAY = 0.95
LEARN_RATE = 0.005
WEIGHT_DECAY = 0.1
ADAM_EPS = 1e-08
AVERAGE_MIX = 0.25
INTERP_BETA = 0.9


def from_behind(block, axis, distance):
    devices = range(lax.axis_size(axis))
    route = [(i - distance, i) for i in devices if i - distance in devices]
    return lax.ppermute(block, axis, route)


def visible(doc_rows, need_row, block_id, tok_rows):
    span_rows = (WIN + 1) * tok_rows
    query_pos = block_id * tok_rows + jnp.arange(tok_rows, dtype=jnp.int32)
    key_pos = (block_id - WIN) * tok_rows + jnp.arange(span_rows, dtype=jnp.int32)
    key_block = block_id - WIN + jnp.arange(span_rows, dtype=jnp.int32) // tok_rows
    listed = jnp.any(need_row[None, :] == key_block[:, None], axis=1)
    return (
        (key_pos[None, :] >= doc_rows[:, None])
        & (key_pos[None, :] <= query_pos[:, None])
        & listed[None, :]
    )


def block_attention(query_rows, key_window, value_window, allowed):
    tok_rows = query_rows.shape[0]
    scaling = 1.0 / math.sqrt(HEAD)
    query_split = query_rows.reshape(tok_rows, KV_HEADS, GROUP, HEAD)
    prob_list = []
    out_list = []
    for kv_head in range(KV_HEADS):
        key_part = key_window[:, kv_head * HEAD : (kv_head + 1) * HEAD]
        value_part = value_window[:, kv_head * HEAD : (kv_head + 1) * HEAD]
        scores = (
            jnp.einsum(
                "tgh,sh->gts", query_split[:, kv_head], key_part, preferred_element_type=jnp.float32
            )
            * scaling
        )
        scores = jnp.where(allowed[None], scores, -jnp.inf)
        largest = jnp.max(scores, axis=-1, keepdims=True)
        weights = jnp.exp(scores - largest)
        probs_low = (weights / jnp.sum(weights, axis=-1, keepdims=True)).astype(jnp.bfloat16)
        prob_list.append(probs_low)
        out_list.append(
            jnp.einsum("gts,sh->tgh", probs_low, value_part, preferred_element_type=jnp.float32)
        )
    attended = jnp.stack(out_list, axis=1).reshape(tok_rows, KV_HEADS * GROUP * HEAD)
    return (prob_list, attended)


def norm_backward(attended, cot_rows, token_total):
    square_mean = jnp.mean(attended * attended, axis=-1, keepdims=True) + NORM_EPS
    root_scale = jnp.sqrt(square_mean)
    normed = attended / root_scale
    upstream = cot_rows.astype(jnp.float32) / token_total
    inner = jnp.mean(upstream * normed, axis=-1, keepdims=True)
    return ((upstream - normed * inner) / root_scale).astype(jnp.bfloat16)


def window_grads(prob_list, out_grad):
    tok_rows = out_grad.shape[0]
    grad_split = out_grad.reshape(tok_rows, KV_HEADS, GROUP, HEAD)
    head_parts = []
    for kv_head in range(KV_HEADS):
        head_parts.append(
            jnp.einsum(
                "gts,tgh->sh",
                prob_list[kv_head],
                grad_split[:, kv_head],
                preferred_element_type=jnp.float32,
            )
        )
    return jnp.concatenate(head_parts, axis=1)


def on_device(
    embeds,
    queries,
    key_heads,
    cotangent,
    doc_start,
    need_ids,
    y_weight,
    z_weight,
    x_weight,
    second_moment,
):
    tokens_here = embeds[0]
    tok_rows = tokens_here.shape[0]
    kv_width = key_heads.shape[2]
    block_id = lax.axis_index("cp")
    token_total = tok_rows * lax.axis_size("cp") * lax.axis_size("fs")
    columns = tokens_here
    values = jnp.dot(
        columns,
        lax.all_gather(y_weight, ("cp", "fs"), axis=0, tiled=True),
        preferred_element_type=jnp.float32,
    ).astype(jnp.bfloat16)
    paired = jnp.concatenate([key_heads[0], values], axis=1)
    fetched = [paired]
    for offset in range(1, WIN + 1):
        fetched.append(from_behind(paired, "cp", offset))
    stacked = jnp.stack(fetched)
    window = stacked[::-1].reshape((WIN + 1) * tok_rows, 2 * kv_width)
    allowed = visible(doc_start[0], need_ids[0, 0], block_id, tok_rows)
    prob_list, attended = block_attention(
        queries[0], window[:, :kv_width], window[:, kv_width:], allowed
    )
    out_grad = norm_backward(attended, cotangent[0], token_total)
    shares = window_grads(prob_list, out_grad).reshape(WIN + 1, tok_rows, kv_width)[::-1]
    grad_total = shares[0]
    for offset in range(1, WIN + 1):
        grad_total = grad_total + from_behind(shares[offset], "cp", -offset)
    value_grad = grad_total.astype(jnp.bfloat16)
    own_rows = y_weight.shape[0]
    fs_count = lax.axis_size("fs")
    cp_count = lax.axis_size("cp")
    split_cols = tokens_here.reshape(tok_rows, cp_count, fs_count * own_rows)
    exchanged = lax.all_to_all(split_cols, "fs", split_axis=2, concat_axis=0, tiled=True)
    group_cols = exchanged.reshape(fs_count * tok_rows, cp_count * own_rows)
    group_grads = lax.all_gather(value_grad, "fs", axis=0, tiled=True)
    columns = group_cols
    gradient = lax.psum_scatter(
        lax.dot_general(
            columns, group_grads, (((0,), (0,)), ((), ())), preferred_element_type=jnp.float32
        ),
        "cp",
        scatter_dimension=0,
        tiled=True,
    )
    moment_next = MOMENT_DECAY * second_moment + (1.0 - MOMENT_DECAY) * gradient * gradient
    z_next = z_weight - LEARN_RATE * (
        gradient / (jnp.sqrt(moment_next) + ADAM_EPS) + WEIGHT_DECAY * y_weight.astype(jnp.float32)
    )
    x_next = (1.0 - AVERAGE_MIX) * x_weight + AVERAGE_MIX * z_next
    y_next = ((1.0 - INTERP_BETA) * z_next + INTERP_BETA * x_next).astype(jnp.bfloat16)
    return (z_next, x_next, moment_next, y_next)


def solution(mesh):
    return jax.shard_map(
        on_device,
        mesh=mesh,
        in_specs=(
            P("fs", "cp", None),
            P("fs", "cp", None),
            P("fs", "cp", None),
            P("fs", "cp", None),
            P("fs", "cp"),
            P("fs", "cp", None),
            P(("cp", "fs"), None),
            P(("cp", "fs"), None),
            P(("cp", "fs"), None),
            P(("cp", "fs"), None),
        ),
        out_specs=(
            P(("cp", "fs"), None),
            P(("cp", "fs"), None),
            P(("cp", "fs"), None),
            P(("cp", "fs"), None),
        ),
        check_vma=False,
    )
```

profile of v0, /device:TPU:0, one launch (start us, length us, event | category | flops | bytes accessed | tf_op | source)
XLA Modules:
  0.0 381.0 jit_solution(14984176034522954086)
XLA Ops:
  10.2 65.1 %all-gather.3.cloned.1.call-done = bf16[4096,512]{1,0:T(8,128)(2,1)} async-done(((bf16[128,512]{1,0:T(8,128)(2,1)}), bf16[4096,512]{1,0:T(8,128)(2,1)}) %all-gather.3.cloned.1.call-update) | async-done | bytes 4194320 | tf_op jit(solution)/shard_map/all_gather | solution.py:114
  75.3 4.1 %fusion.17 = bf16[256,512]{1,0:T(8,128)(2,1)S(1)} fusion(bf16[4096,512]{1,0:T(8,128)(2,1)} %all-gather.3.cloned.1.call-done, bf16[1,256,4096]{2,1,0:T(8,128)(2,1)} %param.10), kind=kOutput, calls=%fused_computation.42 | convolution fusion | flops 1073872896 | bytes 6553600 | tf_op jit(solution)/shard_map/dot_general | solution.py:112
  81.0 4.2 %collective-permute-start = (bf16[256,1024]{1,0:T(8,128)(2,1)}, bf16[256,1024]{1,0:T(8,128)(2,1)}, u32[]{:S(2)}, u32[]{:S(2)}) collective-permute-start(bf16[256,1024]{1,0:T(8,128)(2,1)} %pad_maximum_fusion.2), channel_id=1, source_target_pairs={{0,4},{4,8},{8,12},{12,16},{16,20},{20,24},{24,28},{1,5},{5,9},{9,... | collective-permute-start | bytes 1572872 | tf_op jit(solution)/shard_map/ppermute | solution.py:26
  85.1 3.3 collective-permute-start.1
  91.4 1.9 copy.184
  93.2 2.4 collective-permute-start.2
  96.5 2.1 collective-permute-start.3
  98.7 1.9 bitcast_dynamic-update-slice_fusion.3
  100.5 1.9 bitcast_dynamic-update-slice_fusion.2
  102.4 9.1 %collective-permute-done.2 = bf16[256,1024]{1,0:T(8,128)(2,1)S(1)} collective-permute-done((bf16[256,1024]{1,0:T(8,128)(2,1)}, bf16[256,1024]{1,0:T(8,128)(2,1)S(1)}, u32[]{:S(2)}, u32[]{:S(2)}) %collective-permute-start.2) | collective-permute-done | bytes 524320 | tf_op jit(solution)/shard_map/ppermute | solution.py:26
  112.4 9.4 %collective-permute-done.3 = bf16[256,1024]{1,0:T(8,128)(2,1)S(1)} collective-permute-done((bf16[256,1024]{1,0:T(8,128)(2,1)}, bf16[256,1024]{1,0:T(8,128)(2,1)S(1)}, u32[]{:S(2)}, u32[]{:S(2)}) %collective-permute-start.3) | collective-permute-done | bytes 524320 | tf_op jit(solution)/shard_map/ppermute | solution.py:26
  122.6 2.0 rev.4
  124.7 5.2 %exponential_reduce_fusion.3 = (f32[4,256]{1,0:T(4,128)S(1)}, f32[4,256,1280]{1,2,0:T(8,128)}) fusion(pred[256,1280]{0,1:T(8,128)(4,1)S(1)} %copy-done.19, bf16[1280,1024]{1,0:T(8,128)(2,1)S(1)} %bitcast.201, bf16[256,4,4,128]{0,3,2,1:T(8,128)(2,1)} %bitcast.214), kind=kOutput, calls=%fused_computation.19 | convolution fusion | flops 340788480 | bytes 6164480 | tf_op jit(solution)/shard_map/sub | solution.py:59
  129.9 5.1 %exponential_reduce_fusion.2 = (f32[4,256]{1,0:T(4,128)S(1)}, f32[4,256,1280]{1,2,0:T(8,128)}) fusion(pred[256,1280]{0,1:T(8,128)(4,1)S(1)} %copy-done.19, bf16[1280,1024]{1,0:T(8,128)(2,1)S(1)} %bitcast.202, bf16[256,4,4,128]{0,3,2,1:T(8,128)(2,1)} %bitcast.215), kind=kOutput, calls=%fused_computation.18 | convolution fusion | flops 340788480 | bytes 6164480 | tf_op jit(solution)/shard_map/sub | solution.py:59
  135.0 5.1 %exponential_reduce_fusion.1 = (f32[4,256]{1,0:T(4,128)S(1)}, f32[4,256,1280]{1,2,0:T(8,128)}) fusion(pred[256,1280]{0,1:T(8,128)(4,1)S(1)} %copy-done.19, bf16[1280,1024]{1,0:T(8,128)(2,1)S(1)} %bitcast.203, bf16[256,4,4,128]{0,3,2,1:T(8,128)(2,1)} %bitcast.216), kind=kOutput, calls=%fused_computation.17 | convolution fusion | flops 340788480 | bytes 6164480 | tf_op jit(solution)/shard_map/sub | solution.py:59
  140.1 5.1 %exponential_reduce_fusion = (f32[4,256]{1,0:T(4,128)S(1)}, f32[4,256,1280]{1,2,0:T(8,128)}) fusion(pred[256,1280]{0,1:T(8,128)(4,1)S(1)} %copy-done.19, bf16[1280,1024]{1,0:T(8,128)(2,1)S(1)} %bitcast.204, bf16[256,4,4,128]{0,3,2,1:T(8,128)(2,1)} %bitcast.217), kind=kOutput, calls=%fused_computation.16 | convolution fusion | flops 340788480 | bytes 6164480 | tf_op jit(solution)/shard_map/sub | solution.py:59
  145.1 4.0 %divide_convert_fusion.3 = bf16[4,256,1280]{1,2,0:T(8,128)(2,1)S(1)} fusion(f32[4,256,1280]{1,2,0:T(8,128)} %get-tuple-element.48, f32[4,256]{1,0:T(4,128)S(1)} %get-tuple-element.47), kind=kLoop, calls=%fused_computation.15 | loop fusion | flops 2621440 | bytes 7868416 | tf_op jit(solution)/shard_map/convert_element_type | solution.py:60
  149.7 4.0 %divide_convert_fusion.2 = bf16[4,256,1280]{1,2,0:T(8,128)(2,1)S(1)} fusion(f32[4,256,1280]{1,2,0:T(8,128)} %get-tuple-element.46, f32[4,256]{1,0:T(4,128)S(1)} %get-tuple-element.45), kind=kLoop, calls=%fused_computation.14 | loop fusion | flops 2621440 | bytes 7868416 | tf_op jit(solution)/shard_map/convert_element_type | solution.py:60
  162.0 2.9 copy.196
  164.9 2.5 fusion.11
  182.1 4.1 %copy.201 = bf16[1,256,4096]{1,2,0:T(8,128)(2,1)} copy(bf16[1,256,4096]{2,1,0:T(8,128)(2,1)} %param.10) | data formatting | bytes 4194304 | tf_op args[0]
  186.2 4.1 %copy.202 = bf16[256,8,512]{0,1,2:T(8,128)(2,1)} copy(bf16[256,8,512]{0,2,1:T(8,128)(2,1)} %bitcast.200) | data formatting | bytes 4194304 | tf_op jit(solution)/shard_map/reshape;squeeze | solution.py:136
  190.3 4.4 %all-to-all-start = ((bf16[256,8,512]{0,1,2:T(8,128)(2,1)}), bf16[256,8,512]{0,1,2:T(8,128)(2,1)}, u32[]{:S(2)}, u32[]{:S(2)}) async-start(bf16[256,8,512]{0,1,2:T(8,128)(2,1)} %copy.202), calls=%async_computation | async-start | bytes 4194304 | tf_op jit(solution)/shard_map/all_to_all | solution.py:137
  194.8 5.3 %collective-permute-done.4 = f32[256,512]{0,1:T(8,128)S(1)} collective-permute-done((f32[256,512]{0,1:T(8,128)}, f32[256,512]{0,1:T(8,128)S(1)}, u32[]{:S(2)}, u32[]{:S(2)}) %collective-permute-start.4) | collective-permute-done | bytes 524320 | tf_op jit(solution)/shard_map/ppermute | solution.py:26
  200.1 13.4 %collective-permute-done.5 = f32[256,512]{0,1:T(8,128)} collective-permute-done((f32[256,512]{0,1:T(8,128)}, f32[256,512]{0,1:T(8,128)}, u32[]{:S(2)}, u32[]{:S(2)}) %collective-permute-start.5) | collective-permute-done | bytes 524320 | tf_op jit(solution)/shard_map/ppermute | solution.py:26
  213.5 22.8 %collective-permute-done.6 = f32[256,512]{0,1:T(8,128)} collective-permute-done((f32[256,512]{0,1:T(8,128)}, f32[256,512]{0,1:T(8,128)}, u32[]{:S(2)}, u32[]{:S(2)}) %collective-permute-start.6) | collective-permute-done | bytes 524320 | tf_op jit(solution)/shard_map/ppermute | solution.py:26
  236.3 43.8 %collective-permute-done.7 = f32[256,512]{0,1:T(8,128)} collective-permute-done((f32[256,512]{0,1:T(8,128)}, f32[256,512]{0,1:T(8,128)}, u32[]{:S(2)}, u32[]{:S(2)}) %collective-permute-start.7) | collective-permute-done | bytes 524320 | tf_op jit(solution)/shard_map/ppermute | solution.py:26
  280.2 2.2 fusion.23
  282.4 3.9 %copy.203 = bf16[256,8,512]{2,1,0:T(8,128)(2,1)S(1)} copy(bf16[256,8,512]{0,1,2:T(8,128)(2,1)} %all-to-all-done) | data formatting | bytes 4194304 | tf_op jit(solution)/shard_map/all_to_all | solution.py:137
  288.0 8.4 %all-gather.5.cloned.1.call-done = bf16[1024,512]{0,1:T(8,128)(2,1)} async-done(((bf16[256,512]{0,1:T(8,128)(2,1)}), bf16[1024,512]{0,1:T(8,128)(2,1)}) %all-gather.5.cloned.1.call-update) | async-done | bytes 1048592 | tf_op jit(solution)/shard_map/all_gather | solution.py:139
  296.4 4.5 %fusion.14 = f32[1024,512]{0,1:T(8,128)} fusion(bf16[1024,512]{0,1:T(8,128)(2,1)} %all-gather.5.cloned.1.call-done, bf16[128,8,8,128]{3,2,1,0:T(8,128)(2,1)} %bitcast.213), kind=kOutput, calls=%fused_computation.36 | convolution fusion | flops 1073741824 | bytes 5242880 | tf_op jit(solution)/shard_map/dot_general | solution.py:142
  302.1 67.9 %reduce-scatter.2.cloned.1.call-done = f32[128,512]{0,1:T(8,128)} async-done(((f32[1024,512]{0,1:T(8,128)}), f32[128,512]{0,1:T(8,128)}) %reduce-scatter.2.cloned.1.call-update) | async-done | bytes 262160 | tf_op jit(solution)/shard_map/reduce_scatter | solution.py:141
  (109 shorter events, 40.8 us)
Async XLA Ops:
  7.2 68.1 %all-gather.3.cloned.1.call-start = ((), (), s32[]{:S(2)}) async-start(), calls=%async_computation.2 | async-start | bytes 4325376 | tf_op jit(solution)/shard_map/all_gather | solution.py:114
  10.2 69.9 %copy-start.15 = (bf16[1,256,512]{2,1,0:T(8,128)(2,1)S(1)}, bf16[1,256,512]{2,1,0:T(8,128)(2,1)}, u32[]{:S(2)}) copy-start(bf16[1,256,512]{2,1,0:T(8,128)(2,1)} %param.12) | copy-start | bytes 786436
  10.2 78.3 %copy-start.23 = (s32[1,256]{1,0:T(1,128)S(1)}, s32[1,256]{1,0:T(1,128)}, u32[]{:S(2)}) copy-start(s32[1,256]{1,0:T(1,128)} %param.14) | copy-start | bytes 3076
  10.2 79.9 %copy-start.14 = (bf16[1,256,2048]{2,1,0:T(8,128)(2,1)S(1)}, bf16[1,256,2048]{2,1,0:T(8,128)(2,1)}, u32[]{:S(2)}) copy-start(bf16[1,256,2048]{2,1,0:T(8,128)(2,1)} %param.11) | copy-start | bytes 3145732
  81.0 17.7 %collective-permute-start = (bf16[256,1024]{1,0:T(8,128)(2,1)}, bf16[256,1024]{1,0:T(8,128)(2,1)}, u32[]{:S(2)}, u32[]{:S(2)}) collective-permute-start(bf16[256,1024]{1,0:T(8,128)(2,1)} %pad_maximum_fusion.2), channel_id=1, source_target_pairs={{0,4},{4,8},{8,12},{12,16},{16,20},{20,24},{24,28},{1,5},{5,9},{9,... | collective-permute-start | bytes 1572872 | tf_op jit(solution)/shard_map/ppermute | solution.py:26
  85.1 15.4 %collective-permute-start.1 = (bf16[256,1024]{1,0:T(8,128)(2,1)}, bf16[256,1024]{1,0:T(8,128)(2,1)}, u32[]{:S(2)}, u32[]{:S(2)}) collective-permute-start(bf16[256,1024]{1,0:T(8,128)(2,1)} %pad_maximum_fusion.2), channel_id=1, source_target_pairs={{0,8},{4,12},{8,16},{12,20},{16,24},{20,28},{1,9},{5,13},{9,17},{1... | collective-permute-start | bytes 1572872 | tf_op jit(solution)/shard_map/ppermute | solution.py:26
  91.4 4.3 %copy-start.17 = (bf16[256,512]{1,0:T(8,128)(2,1)S(1)}, bf16[256,512]{1,0:T(8,128)(2,1)}, u32[]{:S(2)}) copy-start(bf16[256,512]{1,0:T(8,128)(2,1)} %copy-done.16) | copy-start | bytes 786436
  93.2 18.3 %collective-permute-start.2 = (bf16[256,1024]{1,0:T(8,128)(2,1)}, bf16[256,1024]{1,0:T(8,128)(2,1)S(1)}, u32[]{:S(2)}, u32[]{:S(2)}) collective-permute-start(bf16[256,1024]{1,0:T(8,128)(2,1)} %pad_maximum_fusion.2), channel_id=1, source_target_pairs={{0,12},{4,16},{8,20},{12,24},{16,28},{1,13},{5,17},{9,21},{13,25},... | collective-permute-start | bytes 1572872 | tf_op jit(solution)/shard_map/ppermute | solution.py:26
  96.5 25.3 %collective-permute-start.3 = (bf16[256,1024]{1,0:T(8,128)(2,1)}, bf16[256,1024]{1,0:T(8,128)(2,1)S(1)}, u32[]{:S(2)}, u32[]{:S(2)}) collective-permute-start(bf16[256,1024]{1,0:T(8,128)(2,1)} %pad_maximum_fusion.2), channel_id=1, source_target_pairs={{0,16},{4,20},{8,24},{12,28},{1,17},{5,21},{9,25},{13,29},{2,18},{... | collective-permute-start | bytes 1572872 | tf_op jit(solution)/shard_map/ppermute | solution.py:26
  124.7 15.4 %copy-start.7 = (bf16[5,256,1024]{2,1,0:T(8,128)(2,1)}, bf16[5,256,1024]{2,1,0:T(8,128)(2,1)S(1)}, u32[]{:S(2)}) copy-start(bf16[5,256,1024]{2,1,0:T(8,128)(2,1)S(1)} %rev.4) | copy-start | bytes 7864324
  145.1 4.0 %copy-start.8 = (bf16[5,256,1024]{2,1,0:T(8,128)(2,1)S(1)}, bf16[5,256,1024]{2,1,0:T(8,128)(2,1)}, u32[]{:S(2)}) copy-start(bf16[5,256,1024]{2,1,0:T(8,128)(2,1)} %copy-done.7) | copy-start | bytes 7864324
  149.7 4.6 %slice-start.2 = ((s8[5242880]{0:T(1024)(128)(4,1)}), s8[4194304]{0:T(1024)(128)(4,1)S(1)}, s32[]{:S(2)}) async-start(s8[5242880]{0:T(1024)(128)(4,1)} %bitcast.211), calls=%async_computation.7 | async-start | bytes 8388608
  149.7 4.6 %slice-start.3 = ((s8[5242880]{0:T(1024)(128)(4,1)}), s8[1048576]{0:T(1024)(128)(4,1)S(1)}, s32[]{:S(2)}) async-start(s8[5242880]{0:T(1024)(128)(4,1)} %bitcast.211), calls=%async_computation.8 | async-start | bytes 2097152
  153.7 2.2 copy-start
  154.2 6.0 %copy-start.9 = (f32[256,1,4,128]{0,3,2,1:T(8,128)}, f32[256,1,4,128]{0,3,2,1:T(8,128)S(1)}, u32[]{:S(2)}) copy-start(f32[256,1,4,128]{0,3,2,1:T(8,128)S(1)} %convolution_bitcast_fusion.6) | copy-start | bytes 1572868
  154.2 2.9 slice-start
  154.3 4.0 %slice-start.1 = ((s8[5242880]{0:T(1024)(128)(4,1)}), s8[1048576]{0:T(1024)(128)(4,1)S(1)}, s32[]{:S(2)}) async-start(s8[5242880]{0:T(1024)(128)(4,1)} %bitcast.209), calls=%async_computation.6 | async-start | bytes 2097152
  155.9 3.8 copy-start.2
  156.5 3.8 copy-start.11
  159.7 2.3 copy-start.4
  164.9 2.5 copy-start.6
  164.9 2.6 copy-start.10
  164.9 2.8 copy-start.12
  176.9 23.2 %collective-permute-start.4 = (f32[256,512]{0,1:T(8,128)}, f32[256,512]{0,1:T(8,128)S(1)}, u32[]{:S(2)}, u32[]{:S(2)}) collective-permute-start(f32[256,512]{0,1:T(8,128)} %get-tuple-element.34), channel_id=1, source_target_pairs={{4,0},{8,4},{12,8},{16,12},{20,16},{24,20},{28,24},{5,1},{9,5},{13... | collective-permute-start | bytes 1572872 | tf_op jit(solution)/shard_map/ppermute | solution.py:26
  178.2 35.3 %collective-permute-start.5 = (f32[256,512]{0,1:T(8,128)}, f32[256,512]{0,1:T(8,128)}, u32[]{:S(2)}, u32[]{:S(2)}) collective-permute-start(f32[256,512]{0,1:T(8,128)} %get-tuple-element.37), channel_id=1, source_target_pairs={{8,0},{12,4},{16,8},{20,12},{24,16},{28,20},{9,1},{13,5},{17,9},{2... | collective-permute-start | bytes 1572872 | tf_op jit(solution)/shard_map/ppermute | solution.py:26
  179.5 56.8 %collective-permute-start.6 = (f32[256,512]{0,1:T(8,128)}, f32[256,512]{0,1:T(8,128)}, u32[]{:S(2)}, u32[]{:S(2)}) collective-permute-start(f32[256,512]{0,1:T(8,128)} %get-tuple-element.36), channel_id=1, source_target_pairs={{12,0},{16,4},{20,8},{24,12},{28,16},{13,1},{17,5},{21,9},{25,13},... | collective-permute-start | bytes 1572872 | tf_op jit(solution)/shard_map/ppermute | solution.py:26
  180.8 99.3 %collective-permute-start.7 = (f32[256,512]{0,1:T(8,128)}, f32[256,512]{0,1:T(8,128)}, u32[]{:S(2)}, u32[]{:S(2)}) collective-permute-start(f32[256,512]{0,1:T(8,128)} %get-tuple-element.35), channel_id=1, source_target_pairs={{16,0},{20,4},{24,8},{28,12},{17,1},{21,5},{25,9},{29,13},{18,2},{... | collective-permute-start | bytes 1572872 | tf_op jit(solution)/shard_map/ppermute | solution.py:26
  190.3 92.1 %all-to-all-start = ((bf16[256,8,512]{0,1,2:T(8,128)(2,1)}), bf16[256,8,512]{0,1,2:T(8,128)(2,1)}, u32[]{:S(2)}, u32[]{:S(2)}) async-start(bf16[256,8,512]{0,1,2:T(8,128)(2,1)} %copy.202), calls=%async_computation | async-start | bytes 4194304 | tf_op jit(solution)/shard_map/all_to_all | solution.py:137
  194.7 101.6 %all-gather.5.cloned.1.call-start = ((), (), s32[]{:S(2)}) async-start(), calls=%async_computation.3 | async-start | bytes 1310720 | tf_op jit(solution)/shard_map/all_gather | solution.py:139
  282.4 87.6 %reduce-scatter.2.cloned.1.call-start = ((), (), s32[]{:S(2)}) async-start(), calls=%async_computation.4 | async-start | bytes 2359296 | tf_op jit(solution)/shard_map/reduce_scatter | solution.py:141
  296.4 4.6 %copy-start.18 = (bf16[128,512]{1,0:T(8,128)(2,1)S(1)}, bf16[128,512]{1,0:T(8,128)(2,1)}, u32[]{:S(2)}) copy-start(bf16[128,512]{1,0:T(8,128)(2,1)} %param.16) | copy-start | bytes 393220
  296.4 4.7 %copy-start.20 = (f32[128,512]{1,0:T(8,128)S(1)}, f32[128,512]{1,0:T(8,128)}, u32[]{:S(2)}) copy-start(f32[128,512]{1,0:T(8,128)} %param.18) | copy-start | bytes 786436
  (8 other events, 11.7 us)
Sparse Core Ops, SparseCore 0:
  10.8 64.4 all-gather.2
  282.5 13.8 all-gather.4
  301.1 68.8 reduce-scatter.1
where the time goes:
time: 382 us; the launch traced here: 381 us
  waiting for transfers between devices  246 us (64%)
  local copies, waits for them, and re-layouts  38.1 us (10%)
  matrix products  35.1 us (9%)
  other arithmetic  25.8 us (7%)
  starting transfers between devices  21.7 us (6%)
  between operations  14.3 us (4%)
    ppermute x8, waiting for transfers between devices, from_behind(): return lax.ppermute(block, axis, route)  104 us
    reduce_scatter x1, waiting for transfers between devices, on_device(): lax.psum_scatter(lax.dot_general(columns, group_grads, (((0,), (0,)), (()...  67.9 us
    all_gather x1, waiting for transfers between devices, on_device(): lax.all_gather(y_weight, ('cp', 'fs'), axis=0, tiled=True)  65.1 us
    sub x4, matrix products, block_attention(): weights = jnp.exp(scores - largest)  20.5 us
    unnamed x69, local copies, waits for them, and re-layouts  19.5 us
    ppermute x8, starting transfers between devices, from_behind(): return lax.ppermute(block, axis, route)  17.2 us
    convert_element_type x4, other arithmetic, block_attention(): (weights / jnp.sum(weights, axis=-1, keepdims=True)).astype(jnp.bfloat16)  11 us
    all_gather x1, waiting for transfers between devices, on_device(): group_grads = lax.all_gather(value_grad, 'fs', axis=0, tiled=True)  8.39 us
  transfers between devices with their start and end apart: 12, of which 9 were waited for; matrix products, arithmetic and copies ran while one was open for 8% of the time, Pallas kernels for 0%

commit v1 on v0

--- a/solution.py
+++ b/solution.py
@@ -3,6 +3,8 @@
 import jax
 import jax.numpy as jnp
 from jax import lax
+from jax.experimental import pallas as pl
+from jax.experimental.pallas import tpu as pltpu
 from jax.sharding import PartitionSpec as P
 
 HEAD = 128
@@ -20,10 +22,449 @@
 INTERP_BETA = 0.9
 
 
-def from_behind(block, axis, distance):
-    devices = range(lax.axis_size(axis))
-    route = [(i - distance, i) for i in devices if i - distance in devices]
-    return lax.ppermute(block, axis, route)
+MESH = pl.DeviceIdType.MESH
+VMEM_LIMIT = 60 * 1024 * 1024
+
+
+def signal_and_wait(peers):
+    barrier = pltpu.get_barrier_semaphore()
+    for peer in peers:
+        pl.semaphore_signal(barrier, inc=1, device_id=peer, device_id_type=MESH)
+    pl.semaphore_wait(barrier, len(peers))
+
+
+def remote(src, dst, send_sem, recv_sem, peer):
+    return pltpu.make_async_remote_copy(
+        src_ref=src,
+        dst_ref=dst,
+        send_sem=send_sem,
+        recv_sem=recv_sem,
+        device_id=peer,
+        device_id_type=MESH,
+    )
+
+
+class Place:
+    def __init__(self, cp_count, fs_count):
+        self.n, self.m = cp_count, fs_count
+        self.c, self.f = lax.axis_index("cp"), lax.axis_index("fs")
+        self.pair, self.side = self.c // 2, self.c % 2
+        self.half = cp_count // 2
+        self.mate_c = self.c + 1 - 2 * self.side
+        self.twin_f = self.f + 1 - 2 * (self.f % 2)
+        self.mate = {"cp": self.mate_c, "fs": self.f}
+        self.twin = {"cp": self.c, "fs": self.twin_f}
+
+    def column_c(self, step):
+        return ((self.pair + step) % self.half) * 2 + self.side
+
+    def column(self, step):
+        return {"cp": self.column_c(step), "fs": self.f}
+
+    def across_f(self, step):
+        return (self.f + 2 * step) % self.m
+
+    def across(self, step):
+        return {"cp": self.c, "fs": self.across_f(step)}
+
+    def columns(self):
+        return [self.column(d) for d in range(1, self.half)]
+
+    def acrosses(self):
+        return [self.across(e) for e in range(1, self.m // 2)]
+
+
+class Window:
+    def __init__(self, place, own, win, send, recv):
+        self.p, self.own, self.win, self.send, self.recv = place, own, win, send, recv
+        self.rows = own.shape[0]
+
+    def slot(self, back):
+        return self.win.at[pl.ds((WIN - back) * self.rows, self.rows)]
+
+    def ahead(self, back):
+        p = self.p
+        peer = {"cp": jnp.minimum(p.c + back, p.n - 1), "fs": p.f}
+        return remote(self.own, self.slot(back), self.send.at[back - 1], self.recv.at[back - 1], peer)
+
+    def to_mate(self, source, back):
+        return remote(source, self.slot(back), self.send.at[back - 1], self.recv.at[back - 1], self.p.mate)
+
+    def begin(self):
+        p = self.p
+        for back in (4, 2):
+
+            @pl.when(p.c + back < p.n)
+            def _():
+                self.ahead(back).start()
+
+        @pl.when(p.side == 0)
+        def _():
+            self.to_mate(self.own, 1).start()
+
+    def fill(self):
+        p = self.p
+        self.win[pl.ds(WIN * self.rows, self.rows), :] = self.own[...]
+        for back in range(1, WIN + 1):
+
+            @pl.when(p.c < back)
+            def _():
+                self.win[pl.ds((WIN - back) * self.rows, self.rows), :] = jnp.zeros(
+                    self.own.shape, self.own.dtype
+                )
+
+    def relay(self):
+        p = self.p
+
+        @pl.when(p.c >= 2)
+        def _():
+            self.ahead(2).wait_recv()
+
+        @pl.when((p.c >= 2) & (p.side == 1))
+        def _():
+            self.to_mate(self.slot(2), 1).start()
+
+        @pl.when((p.c >= 2) & (p.side == 0))
+        def _():
+            self.to_mate(self.slot(2), 3).start()
+
+        @pl.when(p.c >= 4)
+        def _():
+            self.ahead(4).wait_recv()
+
+        @pl.when((p.c >= 4) & (p.side == 1))
+        def _():
+            self.to_mate(self.slot(4), 3).start()
+
+    def end(self):
+        p = self.p
+        for back in (1, 3):
+
+            @pl.when(p.c >= back)
+            def _():
+                self.to_mate(self.own, back).wait_recv()
+
+        for back in (2, 4):
+
+            @pl.when(p.c + back < p.n)
+            def _():
+                self.ahead(back).wait_send()
+
+        @pl.when((p.side == 0) | (p.c >= 2))
+        def _():
+            self.to_mate(self.own, 1).wait_send()
+
+        @pl.when(((p.side == 0) & (p.c >= 2)) | (p.c >= 4))
+        def _():
+            self.to_mate(self.own, 3).wait_send()
+
+
+def weight_kernel(n, m, y_ref, k_ref, full_ref, win_ref, send, recv, wsend, wrecv):
+    p = Place(n, m)
+    rows = y_ref.shape[0]
+    half, far = n // 2, m // 2
+    signal_and_wait(p.columns() + [p.mate] + p.acrosses() + [p.twin])
+
+    def slot(c, f):
+        return full_ref.at[pl.ds(pl.multiple_of((c * m + f) * rows, rows), rows)]
+
+    mate_base = half
+    across_base = mate_base + half
+    twin_base = across_base + (far - 1) * n
+    pending = []
+
+    def push(source, c, f, number, peer):
+        copy = remote(source, slot(c, f), send.at[number], recv.at[number], peer)
+        copy.start()
+        pending.append(copy)
+
+    def arrive(c, f, number):
+        remote(slot(c, f), slot(c, f), send.at[number], recv.at[number], p.mate).wait_recv()
+
+    def spread(source, c, order):
+        for e in range(1, far):
+            push(source, c, p.f, across_base + (e - 1) * n + order, p.across(e))
+        push(source, c, p.f, twin_base + order, p.twin)
+
+    for d in range(1, half):
+        push(y_ref, p.c, p.f, d, p.column(d))
+    push(y_ref, p.c, p.f, mate_base, p.mate)
+    spread(y_ref, p.c, 0)
+    window = Window(p, k_ref, win_ref, wsend, wrecv)
+    window.begin()
+    full_ref[pl.ds(pl.multiple_of((p.c * m + p.f) * rows, rows), rows), :] = y_ref[...]
+    window.fill()
+    for d in range(half):
+        if d > 0:
+            from_c = p.column_c(half - d)
+            arrive(from_c, p.f, d)
+            push(slot(from_c, p.f), from_c, p.f, mate_base + d, p.mate)
+            spread(slot(from_c, p.f), from_c, 2 * d)
+        mate_c = p.column_c(half - d) + 1 - 2 * p.side
+        arrive(mate_c, p.f, mate_base + d)
+        spread(slot(mate_c, p.f), mate_c, 2 * d + 1)
+    window.relay()
+
+    def ordered(order):
+        from_c = p.column_c((half - order // 2) % half)
+        return from_c if order % 2 == 0 else from_c + 1 - 2 * p.side
+
+    for order in range(n):
+        c = ordered(order)
+        for e in range(1, far):
+            g = (p.f + m - 2 * e) % m
+            number = across_base + (e - 1) * n + order
+            arrive(c, g, number)
+            push(slot(c, g), c, g, twin_base + n + (e - 1) * n + order, p.twin)
+    for order in range(n):
+        c = ordered(order)
+        arrive(c, p.twin_f, twin_base + order)
+        for e in range(1, far):
+            g = (p.twin_f + m - 2 * e) % m
+            arrive(c, g, twin_base + n + (e - 1) * n + order)
+    window.end()
+    for copy in pending:
+        copy.wait_send()
+
+
+def gather_weight(y_weight, keys, n, m):
+    rows, width = y_weight.shape
+    tok_rows = keys.shape[0]
+    numbers = n + (m // 2 - 1) * n + (m // 2) * n
+    return pl.pallas_call(
+        lambda *refs: weight_kernel(n, m, *refs),
+        out_shape=(
+            jax.ShapeDtypeStruct((rows * n * m, width), y_weight.dtype),
+            jax.ShapeDtypeStruct(((WIN + 1) * tok_rows, width), keys.dtype),
+        ),
+        in_specs=[pl.BlockSpec(memory_space=pltpu.VMEM)] * 2,
+        out_specs=(pl.BlockSpec(memory_space=pltpu.VMEM),) * 2,
+        scratch_shapes=[
+            pltpu.SemaphoreType.DMA((numbers,)),
+            pltpu.SemaphoreType.DMA((numbers,)),
+            pltpu.SemaphoreType.DMA((WIN,)),
+            pltpu.SemaphoreType.DMA((WIN,)),
+        ],
+        compiler_params=pltpu.CompilerParams(
+            collective_id=1, has_side_effects=True, vmem_limit_bytes=VMEM_LIMIT
+        ),
+        name="gather_weight",
+    )(y_weight, keys)
+
+
+def column_kernel(n, m, v_ref, e_ref, win_ref, cols_ref, send, recv, wsend, wrecv):
+    p = Place(n, m)
+    strips, _, _, wide = cols_ref.shape
+    others = [{"cp": p.c, "fs": (p.f + e) % m} for e in range(1, m)]
+    signal_and_wait(p.columns() + [p.mate] + others)
+    window = Window(p, v_ref, win_ref, wsend, wrecv)
+    window.begin()
+
+    def strip(k, f):
+        return pl.ds(pl.multiple_of((k * m + f) * wide, wide), wide)
+
+    pending = []
+    for k in range(strips):
+        for e in range(1, m):
+            copy = remote(
+                e_ref.at[:, strip(k, (p.f + e) % m)],
+                cols_ref.at[k, p.f],
+                send.at[k * (m - 1) + e - 1],
+                recv.at[k * (m - 1) + e - 1],
+                others[e - 1],
+            )
+            copy.start()
+            pending.append(copy)
+    window.fill()
+    for k in range(strips):
+        cols_ref[k, p.f] = e_ref[:, strip(k, p.f)]
+    window.relay()
+    window.end()
+    for k in range(strips):
+        for e in range(1, m):
+            g = (p.f + m - e) % m
+            number = k * (m - 1) + e - 1
+            remote(
+                cols_ref.at[k, g], cols_ref.at[k, g], send.at[number], recv.at[number], others[0]
+            ).wait_recv()
+    for copy in pending:
+        copy.wait_send()
+
+
+def exchange_columns(values, embeds, strips, wide, n, m):
+    tok_rows, width = values.shape
+    copies = strips * (m - 1)
+    return pl.pallas_call(
+        lambda *refs: column_kernel(n, m, *refs),
+        out_shape=(
+            jax.ShapeDtypeStruct(((WIN + 1) * tok_rows, width), values.dtype),
+            jax.ShapeDtypeStruct((strips, m, tok_rows, wide), embeds.dtype),
+        ),
+        in_specs=[pl.BlockSpec(memory_space=pltpu.VMEM)] * 2,
+        out_specs=(pl.BlockSpec(memory_space=pltpu.VMEM),) * 2,
+        scratch_shapes=[
+            pltpu.SemaphoreType.DMA((copies,)),
+            pltpu.SemaphoreType.DMA((copies,)),
+            pltpu.SemaphoreType.DMA((WIN,)),
+            pltpu.SemaphoreType.DMA((WIN,)),
+        ],
+        compiler_params=pltpu.CompilerParams(
+            collective_id=2, has_side_effects=True, vmem_limit_bytes=VMEM_LIMIT
+        ),
+        name="exchange_columns",
+    )(values, embeds)
+
+
+CHUNKS = 2
+
+
+def return_kernel(n, m, own_ref, share_ref, all_ref, got, send, recv, gsend, grecv):
+    p = Place(n, m)
+    tok_rows = own_ref.shape[0]
+    part = tok_rows // CHUNKS
+    far = m // 2
+    around = []
+    for back in range(1, WIN + 1):
+        around.append({"cp": (p.c + back) % n, "fs": p.f})
+        around.append({"cp": (p.c + n - back) % n, "fs": p.f})
+    signal_and_wait(around + p.acrosses() + [p.twin])
+
+    def share(chunk, back):
+        rows = pl.ds(chunk * part, part)
+        peer = {"cp": jnp.maximum(p.c - back, 0), "fs": p.f}
+        number = chunk * WIN + back - 1
+        return remote(
+            share_ref.at[back - 1, rows], got.at[back - 1, rows], send.at[number], recv.at[number], peer
+        )
+
+    for chunk in range(CHUNKS):
+        for back in (4, 3, 2, 1):
+
+            @pl.when(p.c >= back)
+            def _():
+                share(chunk, back).start()
+
+    for back in range(1, WIN + 1):
+
+        @pl.when(p.c + back >= n)
+        def _():
+            got[back - 1] = jnp.zeros(got.shape[1:], got.dtype)
+
+    def spread(f, chunk, number, peer):
+        piece = all_ref.at[f, pl.ds(chunk * part, part)]
+        return remote(piece, piece, gsend.at[number], grecv.at[number], peer)
+
+    pending = []
+    for chunk in range(CHUNKS):
+        base = chunk * (2 * far - 1)
+        rows = pl.ds(chunk * part, part)
+        for back in range(1, WIN + 1):
+
+            @pl.when(p.c + back < n)
+            def _():
+                share(chunk, back).wait_recv()
+
+        total = own_ref[rows, :]
+        for back in range(1, WIN + 1):
+            total = total + got[back - 1, rows, :].astype(jnp.float32)
+        all_ref[p.f, rows, :] = total.astype(all_ref.dtype)
+        for e in range(1, far):
+            pending.append(spread(p.f, chunk, base + e - 1, p.across(e)))
+            pending[-1].start()
+        pending.append(spread(p.f, chunk, base + far - 1, p.twin))
+        pending[-1].start()
+    for chunk in range(CHUNKS):
+        base = chunk * (2 * far - 1)
+        for e in range(1, far):
+            g = (p.f + m - 2 * e) % m
+            spread(g, chunk, base + e - 1, p.twin).wait_recv()
+            pending.append(spread(g, chunk, base + far - 1 + e, p.twin))
+            pending[-1].start()
+    for chunk in range(CHUNKS):
+        base = chunk * (2 * far - 1)
+        for e in range(far):
+            g = (p.twin_f + m - 2 * e) % m
+            spread(g, chunk, base + far - 1 + e, p.twin).wait_recv()
+    for copy in pending:
+        copy.wait_send()
+    for chunk in range(CHUNKS):
+        for back in range(1, WIN + 1):
+
+            @pl.when(p.c >= back)
+            def _():
+                share(chunk, back).wait_send()
+
+
+def return_shares(own, shares, n, m):
+    tok_rows, width = own.shape
+    gathers = CHUNKS * (m - 1)
+    return pl.pallas_call(
+        lambda *refs: return_kernel(n, m, *refs),
+        out_shape=jax.ShapeDtypeStruct((m, tok_rows, width), jnp.bfloat16),
+        in_specs=[pl.BlockSpec(memory_space=pltpu.VMEM)] * 2,
+        out_specs=pl.BlockSpec(memory_space=pltpu.VMEM),
+        scratch_shapes=[
+            pltpu.VMEM(shares.shape, shares.dtype),
+            pltpu.SemaphoreType.DMA((CHUNKS * WIN,)),
+            pltpu.SemaphoreType.DMA((CHUNKS * WIN,)),
+            pltpu.SemaphoreType.DMA((gathers,)),
+            pltpu.SemaphoreType.DMA((gathers,)),
+        ],
+        compiler_params=pltpu.CompilerParams(
+            collective_id=3, has_side_effects=True, vmem_limit_bytes=VMEM_LIMIT
+        ),
+        name="return_shares",
+    )(own, shares)
+
+
+def reduce_kernel(n, m, part_ref, out_ref, mate_got, sums, got, msend, mrecv, send, recv):
+    p = Place(n, m)
+    half = n // 2
+    signal_and_wait(p.columns() + [p.mate])
+
+    def to_mate(d):
+        target = p.column_c(d) + 1 - 2 * p.side
+        return remote(part_ref.at[target], mate_got.at[d], msend.at[d], mrecv.at[d], p.mate)
+
+    def to_owner(d):
+        return remote(sums.at[d], got.at[d], send.at[d], recv.at[d], p.column(d))
+
+    steps = list(range(half // 2, half)) + list(range(half // 2 - 1, 0, -1)) + [0]
+    for d in steps:
+        to_mate(d).start()
+    for d in steps:
+        to_mate(d).wait_recv()
+        both = part_ref[p.column_c(d)].astype(jnp.float32) + mate_got[d].astype(jnp.float32)
+        if d > 0:
+            sums[d] = both.astype(sums.dtype)
+            to_owner(d).start()
+        else:
+            total = both
+    for d in range(1, half):
+        to_owner(d).wait_recv()
+        total = total + got[d].astype(jnp.float32)
+    out_ref[...] = total
+    for d in range(half):
+        to_mate(d).wait_send()
+    for d in range(1, half):
+        to_owner(d).wait_send()
+
+
+def reduce_parts(parts, n, m):
+    _, rows, width = parts.shape
+    half = n // 2
+    return pl.pallas_call(
+        lambda *refs: reduce_kernel(n, m, *refs),
+        out_shape=jax.ShapeDtypeStruct((rows, width), jnp.float32),
+        in_specs=[pl.BlockSpec(memory_space=pltpu.VMEM)],
+        out_specs=pl.BlockSpec(memory_space=pltpu.VMEM),
+        scratch_shapes=[pltpu.VMEM((half, rows, width), parts.dtype)] * 3
+        + [pltpu.SemaphoreType.DMA((half,))] * 4,
+        compiler_params=pltpu.CompilerParams(
+            collective_id=4, has_side_effects=True, vmem_limit_bytes=VMEM_LIMIT
+        ),
+        name="reduce_parts",
+    )(parts)
 
 
 def visible(doc_rows, need_row, block_id, tok_rows):
@@ -108,44 +549,35 @@
     kv_width = key_heads.shape[2]
     block_id = lax.axis_index("cp")
     token_total = tok_rows * lax.axis_size("cp") * lax.axis_size("fs")
-    columns = tokens_here
-    values = jnp.dot(
-        columns,
-        lax.all_gather(y_weight, ("cp", "fs"), axis=0, tiled=True),
+    n, m = lax.axis_size("cp"), lax.axis_size("fs")
+    own_rows = y_weight.shape[0]
+    full_weight, key_window = gather_weight(y_weight, key_heads[0], n, m)
+    values = jnp.dot(tokens_here, full_weight, preferred_element_type=jnp.float32).astype(
+        jnp.bfloat16
+    )
+    if own_rows % 128 == 0:
+        strips, wide, sent_cols = n, own_rows, tokens_here
+    else:
+        strips, wide = 1, n * own_rows
+        sent_cols = (
+            tokens_here.reshape(tok_rows, n, m, own_rows)
+            .transpose(0, 2, 1, 3)
+            .reshape(tok_rows, n * m * own_rows)
+        )
+    value_window, group_cols = exchange_columns(values, sent_cols, strips, wide, n, m)
+    allowed = visible(doc_start[0], need_ids[0, 0], block_id, tok_rows)
+    prob_list, attended = block_attention(queries[0], key_window, value_window, allowed)
+    out_grad = norm_backward(attended, cotangent[0], token_total)
+    shares = window_grads(prob_list, out_grad).reshape(WIN + 1, tok_rows, kv_width)
+    sent_shares = shares[:WIN][::-1].astype(jnp.bfloat16)
+    group_grads = return_shares(shares[WIN], sent_shares, n, m)
+    parts = jnp.einsum(
+        "stw,te->swe",
+        group_cols.reshape(strips, m * tok_rows, wide),
+        group_grads.reshape(m * tok_rows, kv_width),
         preferred_element_type=jnp.float32,
     ).astype(jnp.bfloat16)
-    paired = jnp.concatenate([key_heads[0], values], axis=1)
-    fetched = [paired]
-    for offset in range(1, WIN + 1):
-        fetched.append(from_behind(paired, "cp", offset))
-    stacked = jnp.stack(fetched)
-    window = stacked[::-1].reshape((WIN + 1) * tok_rows, 2 * kv_width)
-    allowed = visible(doc_start[0], need_ids[0, 0], block_id, tok_rows)
-    prob_list, attended = block_attention(
-        queries[0], window[:, :kv_width], window[:, kv_width:], allowed
-    )
-    out_grad = norm_backward(attended, cotangent[0], token_total)
-    shares = window_grads(prob_list, out_grad).reshape(WIN + 1, tok_rows, kv_width)[::-1]
-    grad_total = shares[0]
-    for offset in range(1, WIN + 1):
-        grad_total = grad_total + from_behind(shares[offset], "cp", -offset)
-    value_grad = grad_total.astype(jnp.bfloat16)
-    own_rows = y_weight.shape[0]
-    fs_count = lax.axis_size("fs")
-    cp_count = lax.axis_size("cp")
-    split_cols = tokens_here.reshape(tok_rows, cp_count, fs_count * own_rows)
-    exchanged = lax.all_to_all(split_cols, "fs", split_axis=2, concat_axis=0, tiled=True)
-    group_cols = exchanged.reshape(fs_count * tok_rows, cp_count * own_rows)
-    group_grads = lax.all_gather(value_grad, "fs", axis=0, tiled=True)
-    columns = group_cols
-    gradient = lax.psum_scatter(
-        lax.dot_general(
-            columns, group_grads, (((0,), (0,)), ((), ())), preferred_element_type=jnp.float32
-        ),
-        "cp",
-        scatter_dimension=0,
-        tiled=True,
-    )
+    gradient = reduce_parts(parts.reshape(n, own_rows, kv_width), n, m)
     moment_next = MOMENT_DECAY * second_moment + (1.0 - MOMENT_DECAY) * gradient * gradient
     z_next = z_weight - LEARN_RATE * (
         gradient / (jnp.sqrt(moment_next) + ADAM_EPS) + WEIGHT_DECAY * y_weight.astype(jnp.float32)

time: 382 us -> 232 us (0.61)
  waiting for transfers between devices: 246 us -> 0 us
  Pallas kernels: 0 us -> 148 us
  local copies, waits for them, and re-layouts: 38.1 us -> 14.7 us
  starting transfers between devices: 21.7 us -> 0 us
  between operations: 14.3 us -> 0.96 us
  other arithmetic: 25.8 us -> 29.9 us
    pallas_call x0 -> x4, Pallas kernels: none -> 148 us  [the longest x1 41.3 us: return_shares(): pl.pallas_call(lambda *refs: return_kernel(n, m, *refs), out_shape=jax.Sh...]
    ppermute x8 -> x0, waiting for transfers between devices: 104 us -> none  [from_behind(): return lax.ppermute(block, axis, route)]
    all_gather x2 -> x0, waiting for transfers between devices: 73.5 us -> none  [the longest x1 65.1 us: on_device(): lax.all_gather(y_weight, ('cp', 'fs'), axis=0, tiled=True)]
    reduce_scatter x1 -> x0, waiting for transfers between devices: 67.9 us -> none  [on_device(): lax.psum_scatter(lax.dot_general(columns, group_grads, (((0,), (0,)), (()...]
    ppermute x8 -> x0, starting transfers between devices: 17.2 us -> none  [from_behind(): return lax.ppermute(block, axis, route)]
    unnamed x69 -> x39, local copies, waits for them, and re-layouts: 19.5 us -> 7.61 us
    dot_general x4, matrix products: 2.17 us -> 8.02 us  [block_attention(): jnp.einsum('gts,sh->tgh', probs_low, value_part, preferred_element_type=j...]
    all_to_all x2 -> x0, local copies, waits for them, and re-layouts: 5.53 us -> none  [on_device(): lax.all_to_all(split_cols, 'fs', split_axis=2, concat_axis=0, tiled=True)]
  transfers between devices with their start and end apart: 12 -> 0, of which waited for: 9 -> 0; matrix products, arithmetic and copies ran while one was open for 8% -> 0% of each run, Pallas kernels for 0% -> 0%
where the time goes in v1:
time: 232 us; the launch traced here: 231 us
  Pallas kernels  148 us (64%)
  matrix products  37.8 us (16%)
  other arithmetic  29.9 us (13%)
  local copies, waits for them, and re-layouts  14.7 us (6%)
    pallas_call x1, Pallas kernels, return_shares(): pl.pallas_call(lambda *refs: return_kernel(n, m, *refs), out_shape=jax.Sh...  41.3 us
    pallas_call x1, Pallas kernels, exchange_columns(): pl.pallas_call(lambda *refs: column_kernel(n, m, *refs), out_shape=(jax.S...  41.2 us
    pallas_call x1, Pallas kernels, gather_weight(): pl.pallas_call(lambda *refs: weight_kernel(n, m, *refs), out_shape=(jax.S...  37.3 us
    pallas_call x1, Pallas kernels, reduce_parts(): pl.pallas_call(lambda *refs: reduce_kernel(n, m, *refs), out_shape=jax.Sh...  28 us
    sub x4, matrix products, block_attention(): weights = jnp.exp(scores - largest)  20.9 us
    convert_element_type x4, other arithmetic, block_attention(): (weights / jnp.sum(weights, axis=-1, keepdims=True)).astype(jnp.bfloat16)  15.4 us
    dot_general x4, matrix products, block_attention(): jnp.einsum('gts,sh->tgh', probs_low, value_part, preferred_element_type=j...  8.02 us
    unnamed x39, local copies, waits for them, and re-layouts  7.61 us

profile of v1, /device:TPU:0, one launch (start us, length us, event | category | flops | bytes accessed | tf_op | source)
XLA Modules:
  0.0 231.1 jit_solution(12886608782062210192)
XLA Ops:
  1.4 1.6 and_and_fusion
  3.1 37.3 %gather_weight.1 = (bf16[4096,512]{1,0:T(8,128)(2,1)}, bf16[1280,512]{1,0:T(8,128)(2,1)}) custom-call(bf16[128,512]{1,0:T(8,128)(2,1)} %refs_0_.1, bf16[256,512]{1,0:T(8,128)(2,1)} %bitcast.192), custom_call_target="tpu_custom_call" | custom-call | tf_op jit(solution)/shard_map/gather_weight/pallas_call | solution.py:234
  40.4 1.5 copy.60
  41.9 5.4 %exponential_reduce_fusion.2 = (f32[4,256]{1,0:T(4,128)S(1)}, f32[4,256,1280]{1,2,0:T(8,128)}) fusion(pred[256,1280]{0,1:T(8,128)(4,1)S(1)} %and_and_fusion, bf16[1280,512]{1,0:T(8,128)(2,1)} %get-tuple-element.10, bf16[256,4,4,128]{0,3,2,1:T(8,128)(2,1)S(1)} %bitcast.188), kind=kOutput, calls=%fused_computation.18 | convolution fusion | flops 340788480 | bytes 6164480 | tf_op jit(solution)/shard_map/sub | solution.py:500
  47.2 4.0 %divide_convert_fusion.2 = bf16[4,256,1280]{1,2,0:T(8,128)(2,1)S(1)} fusion(f32[4,256,1280]{1,2,0:T(8,128)} %get-tuple-element.23, f32[4,256]{1,0:T(4,128)S(1)} %get-tuple-element.22), kind=kLoop, calls=%fused_computation.14 | loop fusion | flops 2621440 | bytes 7868416 | tf_op jit(solution)/shard_map/convert_element_type | solution.py:501
  51.6 1.9 fusion.9.refs_0_
  53.5 41.2 %exchange_columns.1 = (bf16[1280,512]{1,0:T(8,128)(2,1)}, bf16[8,4,256,128]{3,2,1,0:T(8,128)(2,1)}) custom-call(bf16[256,512]{1,0:T(8,128)(2,1)} %fusion.9.refs_0_, bf16[256,4096]{1,0:T(8,128)(2,1)} %bitcast.187), custom_call_target="tpu_custom_call" | custom-call | tf_op jit(solution)/shard_map/exchange_columns/pallas_call | solution.py:297
  94.7 1.5 convolution_bitcast_fusion.6
  96.2 5.2 %exponential_reduce_fusion.3 = (f32[4,256]{1,0:T(4,128)S(1)}, f32[4,256,1280]{1,2,0:T(8,128)}) fusion(pred[256,1280]{0,1:T(8,128)(4,1)S(1)} %and_and_fusion, bf16[1280,512]{1,0:T(8,128)(2,1)} %get-tuple-element.10, bf16[256,4,4,128]{0,3,2,1:T(8,128)(2,1)} %bitcast.189), kind=kOutput, calls=%fused_computation.19 | convolution fusion | flops 340788480 | bytes 6164480 | tf_op jit(solution)/shard_map/sub | solution.py:500
  101.4 3.8 %divide_convert_fusion.3 = bf16[4,256,1280]{1,2,0:T(8,128)(2,1)S(1)} fusion(f32[4,256,1280]{1,2,0:T(8,128)} %get-tuple-element.25, f32[4,256]{1,0:T(4,128)S(1)} %get-tuple-element.24), kind=kLoop, calls=%fused_computation.15 | loop fusion | flops 2621440 | bytes 7868416 | tf_op jit(solution)/shard_map/convert_element_type | solution.py:501
  105.2 1.5 copy-done
  106.7 2.3 %convolution_bitcast_fusion.7 = f32[256,1,4,128]{0,3,2,1:T(8,128)} fusion(bf16[4,256,1280]{1,2,0:T(8,128)(2,1)S(1)} %divide_convert_fusion.3, bf16[1280,512]{1,0:T(8,128)(2,1)} %get-tuple-element.11), kind=kOutput, calls=%fused_computation.39 | convolution fusion | flops 335544320 | bytes 3473408 | tf_op jit(solution)/shard_map/gts,sh->tgh/dot_general | solution.py:504
  109.1 5.2 %exponential_reduce_fusion.1 = (f32[4,256]{1,0:T(4,128)S(1)}, f32[4,256,1280]{1,2,0:T(8,128)}) fusion(pred[256,1280]{0,1:T(8,128)(4,1)S(1)} %and_and_fusion, bf16[1280,512]{1,0:T(8,128)(2,1)} %get-tuple-element.10, bf16[256,4,4,128]{0,3,2,1:T(8,128)(2,1)} %bitcast.190), kind=kOutput, calls=%fused_computation.17 | convolution fusion | flops 340788480 | bytes 6164480 | tf_op jit(solution)/shard_map/sub | solution.py:500
  114.2 3.8 %divide_convert_fusion.1 = bf16[4,256,1280]{1,2,0:T(8,128)(2,1)S(1)} fusion(f32[4,256,1280]{1,2,0:T(8,128)} %get-tuple-element.21, f32[4,256]{1,0:T(4,128)S(1)} %get-tuple-element.20), kind=kLoop, calls=%fused_computation.13 | loop fusion | flops 2621440 | bytes 7868416 | tf_op jit(solution)/shard_map/convert_element_type | solution.py:501
  118.1 1.6 copy-done.2
  119.6 2.3 convolution_bitcast_fusion.5
  121.9 5.2 %exponential_reduce_fusion = (f32[4,256]{1,0:T(4,128)S(1)}, f32[4,256,1280]{1,2,0:T(8,128)}) fusion(pred[256,1280]{0,1:T(8,128)(4,1)S(1)} %and_and_fusion, bf16[1280,512]{1,0:T(8,128)(2,1)} %get-tuple-element.10, bf16[256,4,4,128]{0,3,2,1:T(8,128)(2,1)} %bitcast.191), kind=kOutput, calls=%fused_computation.16 | convolution fusion | flops 340788480 | bytes 6164480 | tf_op jit(solution)/shard_map/sub | solution.py:500
  127.1 3.8 %divide_convert_fusion = bf16[4,256,1280]{1,2,0:T(8,128)(2,1)S(1)} fusion(f32[4,256,1280]{1,2,0:T(8,128)} %get-tuple-element.19, f32[4,256]{1,0:T(4,128)S(1)} %get-tuple-element.18), kind=kLoop, calls=%fused_computation.12 | loop fusion | flops 2621440 | bytes 7868416 | tf_op jit(solution)/shard_map/convert_element_type | solution.py:501
  131.0 1.9 convolution_bitcast_fusion.4
  133.2 1.6 multiply_reduce_fusion
  134.8 3.1 %copy.74 = f32[256,2048]{1,0:T(8,128)} copy(f32[256,2048]{0,1:T(8,128)} %bitcast.185) | data formatting | bytes 4194304 | tf_op jit(solution)/shard_map/reshape | solution.py:506
  137.9 2.4 %fusion.8 = f32[256]{0:T(256)S(1)} fusion(f32[256,2048]{1,0:T(8,128)} %copy.74, f32[256]{0:T(256)S(1)} %add_sqrt_fusion, bf16[1,256,2048]{2,1,0:T(8,128)(2,1)} %param.13), kind=kLoop, calls=%fused_computation.30 | loop fusion | flops 2621184 | bytes 3147776 | tf_op jit(solution)/shard_map/reduce_sum | solution.py:515
  140.3 1.6 convert_multiply_fusion
  142.0 2.9 %copy.62 = f32[1,256,2048]{1,2,0:T(8,128)} copy(f32[1,256,2048]{2,1,0:T(8,128)} %convert_multiply_fusion) | data formatting | bytes 4194304 | tf_op jit(solution)/shard_map/div | solution.py:514
  144.8 2.5 %divide_convert_fusion.4 = bf16[256,4,4,128]{0,3,2,1:T(8,128)(2,1)S(1)} fusion(f32[256,4,4,128]{0,3,2,1:T(8,128)} %bitcast.184, f32[256]{0:T(256)S(1)} %broadcast_multiply_fusion, f32[256]{0:T(256)S(1)} %add_sqrt_fusion, f32[256,1,4,128]{0,3,2,1:T(8,128)} %copy-done.9, f32[256,1,4,128]{0,3,2,1:T(8,128)} %convolution_bitcast_fusion.5, ...), kind=kLoop, calls=%fused_computation.32 | loop fusion | flops 4194304 | bytes 5244928 | tf_op jit(solution)/shard_map/convert_element_type | solution.py:516
  151.1 1.1 copy-done.5
  153.2 1.1 rev.5.refs_1_
  154.3 1.7 pad_maximum_fusion.4.refs_0_
  156.1 41.3 %return_shares.1 = bf16[4,256,512]{2,1,0:T(8,128)(2,1)} custom-call(f32[256,512]{1,0:T(8,128)} %pad_maximum_fusion.4.refs_0_, bf16[4,256,512]{2,1,0:T(8,128)(2,1)} %rev.5.refs_1_), custom_call_target="tpu_custom_call" | custom-call | tf_op jit(solution)/shard_map/return_shares/pallas_call | solution.py:401
  197.4 3.6 %bitcast_convert_fusion.refs_0_ = bf16[8,128,512]{2,1,0:T(8,128)(2,1)} fusion(bf16[8,4,256,128]{3,2,1,0:T(8,128)(2,1)S(1)} %copy-done.12, bf16[4,256,512]{2,1,0:T(8,128)(2,1)} %return_shares.1), kind=kOutput, calls=%fused_computation.28 | convolution fusion | flops 1074266112 | bytes 4194304 | tf_op jit(solution)/shard_map/stw,te->swe/dot_general | solution.py:574
  201.0 28.0 %reduce_parts.1 = f32[128,512]{1,0:T(8,128)} custom-call(bf16[8,128,512]{2,1,0:T(8,128)(2,1)} %bitcast_convert_fusion.refs_0_), custom_call_target="tpu_custom_call" | custom-call | tf_op jit(solution)/shard_map/reduce_parts/pallas_call | solution.py:456
  229.1 2.0 add_convert_fusion
  (46 shorter events, 6.2 us)
Async XLA Ops:
  41.8 5.4 %copy-start.13 = (bf16[1,256,2048]{1,2,0:T(8,128)(2,1)}, bf16[1,256,2048]{1,2,0:T(8,128)(2,1)S(1)}, u32[]{:S(2)}) copy-start(bf16[1,256,2048]{1,2,0:T(8,128)(2,1)S(1)} %copy.60) | copy-start | bytes 3145732
  47.2 4.0 %copy-start.11 = (bf16[1,256,4096]{2,1,0:T(8,128)(2,1)S(1)}, bf16[1,256,4096]{2,1,0:T(8,128)(2,1)}, u32[]{:S(2)}) copy-start(bf16[1,256,4096]{2,1,0:T(8,128)(2,1)} %param.10) | copy-start | bytes 6291460
  47.2 4.4 %copy-start.18 = (bf16[4096,512]{1,0:T(8,128)(2,1)S(1)}, bf16[4096,512]{1,0:T(8,128)(2,1)}, u32[]{:S(2)}) copy-start(bf16[4096,512]{1,0:T(8,128)(2,1)} %get-tuple-element.8) | copy-start | bytes 12582916
  105.2 1.5 copy-start
  118.1 1.6 copy-start.2
  130.9 3.8 %copy-start.4 = (bf16[4,256,1280]{1,2,0:T(8,128)(2,1)}, bf16[4,256,1280]{1,2,0:T(8,128)(2,1)S(1)}, u32[]{:S(2)}) copy-start(bf16[4,256,1280]{1,2,0:T(8,128)(2,1)S(1)} %divide_convert_fusion) | copy-start | bytes 7864324
  130.9 1.9 copy-start.7
  131.0 2.2 copy-start.8
  133.2 1.6 copy-start.9
  137.9 2.4 %copy-start.10 = (bf16[1,256,2048]{2,1,0:T(8,128)(2,1)S(1)}, bf16[1,256,2048]{2,1,0:T(8,128)(2,1)}, u32[]{:S(2)}) copy-start(bf16[1,256,2048]{2,1,0:T(8,128)(2,1)} %param.13) | copy-start | bytes 3145732
  144.8 2.8 %copy-start.1 = (bf16[4,256,1280]{1,2,0:T(8,128)(2,1)S(1)}, bf16[4,256,1280]{1,2,0:T(8,128)(2,1)}, u32[]{:S(2)}) copy-start(bf16[4,256,1280]{1,2,0:T(8,128)(2,1)} %copy-done) | copy-start | bytes 7864324
  148.5 1.7 copy-start.3
  150.3 2.8 %copy-start.6 = (f32[1280,128]{1,0:T(8,128)}, f32[1280,128]{1,0:T(8,128)S(1)}, u32[]{:S(2)}) copy-start(f32[1280,128]{1,0:T(8,128)S(1)} %convolution_bitcast_fusion.2) | copy-start | bytes 1966084
  150.3 2.0 copy-start.5
  156.1 41.3 %copy-start.12 = (bf16[8,4,256,128]{3,2,1,0:T(8,128)(2,1)S(1)}, bf16[8,4,256,128]{3,2,1,0:T(8,128)(2,1)}, u32[]{:S(2)}) copy-start(bf16[8,4,256,128]{3,2,1,0:T(8,128)(2,1)} %get-tuple-element.9) | copy-start | bytes 6291460
  197.4 31.7 %copy-start.14 = (bf16[128,512]{1,0:T(8,128)(2,1)S(1)}, bf16[128,512]{1,0:T(8,128)(2,1)}, u32[]{:S(2)}) copy-start(bf16[128,512]{1,0:T(8,128)(2,1)} %refs_0_.1) | copy-start | bytes 393220
  197.4 31.7 %copy-start.15 = (f32[128,512]{1,0:T(8,128)S(1)}, f32[128,512]{1,0:T(8,128)}, u32[]{:S(2)}) copy-start(f32[128,512]{1,0:T(8,128)} %param.18) | copy-start | bytes 786436
  197.4 31.7 %copy-start.16 = (f32[128,512]{1,0:T(8,128)S(1)}, f32[128,512]{1,0:T(8,128)}, u32[]{:S(2)}) copy-start(f32[128,512]{1,0:T(8,128)} %param.17) | copy-start | bytes 786436
  197.4 31.7 %copy-start.17 = (f32[128,512]{1,0:T(8,128)S(1)}, f32[128,512]{1,0:T(8,128)}, u32[]{:S(2)}) copy-start(f32[128,512]{1,0:T(8,128)} %param.19) | copy-start | bytes 786436

commit v2 on v1

--- a/solution.py
+++ b/solution.py
@@ -252,25 +252,65 @@
     )(y_weight, keys)
 
 
-def column_kernel(n, m, v_ref, e_ref, win_ref, cols_ref, send, recv, wsend, wrecv):
+def attend_kernel(
+    n,
+    m,
+    token_total,
+    q_ref,
+    cot_ref,
+    doc_ref,
+    listed_ref,
+    kwin_ref,
+    v_ref,
+    e_ref,
+    cols_ref,
+    all_ref,
+    vwin,
+    bias,
+    probs,
+    att,
+    outg,
+    own,
+    share,
+    got,
+    csend,
+    crecv,
+    wsend,
+    wrecv,
+    send,
+    recv,
+    gsend,
+    grecv,
+):
     p = Place(n, m)
     strips, _, _, wide = cols_ref.shape
+    tok_rows, span_rows = bias.shape
+    heads = KV_HEADS * GROUP
+    far = m // 2
     others = [{"cp": p.c, "fs": (p.f + e) % m} for e in range(1, m)]
-    signal_and_wait(p.columns() + [p.mate] + others)
-    window = Window(p, v_ref, win_ref, wsend, wrecv)
+    around = []
+    for back in range(1, WIN + 1):
+        around.append({"cp": (p.c + back) % n, "fs": p.f})
+        around.append({"cp": (p.c + n - back) % n, "fs": p.f})
+    signal_and_wait(around + others)
+    window = Window(p, v_ref, vwin, wsend, wrecv)
     window.begin()
 
     def strip(k, f):
         return pl.ds(pl.multiple_of((k * m + f) * wide, wide), wide)
+
+    def lanes(h):
+        return pl.ds(pl.multiple_of(h * HEAD, HEAD), HEAD)
 
     pending = []
     for k in range(strips):
         for e in range(1, m):
+            number = k * (m - 1) + e - 1
             copy = remote(
                 e_ref.at[:, strip(k, (p.f + e) % m)],
                 cols_ref.at[k, p.f],
-                send.at[k * (m - 1) + e - 1],
-                recv.at[k * (m - 1) + e - 1],
+                csend.at[number],
+                crecv.at[number],
                 others[e - 1],
             )
             copy.start()
@@ -278,143 +318,180 @@
     window.fill()
     for k in range(strips):
         cols_ref[k, p.f] = e_ref[:, strip(k, p.f)]
+    for back in range(1, WIN + 1):
+
+        @pl.when(p.c + back >= n)
+        def _():
+            got[back - 1] = jnp.zeros(got.shape[1:], got.dtype)
+
+    row = lax.broadcasted_iota(jnp.int32, (tok_rows, span_rows), 0)
+    col = lax.broadcasted_iota(jnp.int32, (tok_rows, span_rows), 1)
+    key_pos = (p.c - WIN) * tok_rows + col
+    seen = (key_pos >= doc_ref[...]) & (key_pos <= p.c * tok_rows + row) & (listed_ref[...] > 0)
+    bias[...] = jnp.where(seen, 0.0, -1e30)
+    rate = math.log2(math.e) / math.sqrt(HEAD)
+
+    def prob_step(h, carry):
+        raw = (
+            lax.dot_general(
+                q_ref[:, lanes(h)],
+                kwin_ref[:, lanes(h // GROUP)],
+                (((1,), (1,)), ((), ())),
+                preferred_element_type=jnp.float32,
+            )
+            + bias[...]
+        )
+        weights = jnp.exp2((raw - jnp.max(raw, axis=1, keepdims=True)) * rate)
+        probs[h] = (weights * (1.0 / jnp.sum(weights, axis=1, keepdims=True))).astype(probs.dtype)
+        return carry
+
+    lax.fori_loop(0, heads * 5 // 8, prob_step, 0)
     window.relay()
+    lax.fori_loop(heads * 5 // 8, heads, prob_step, 0)
     window.end()
+
+    def out_step(h, carry):
+        att[:, lanes(h)] = jnp.dot(
+            probs[h], vwin[:, lanes(h // GROUP)], preferred_element_type=jnp.float32
+        )
+        return carry
+
+    lax.fori_loop(0, heads, out_step, 0)
+    tile = 32
+
+    def norm_step(i, carry):
+        rows = pl.ds(pl.multiple_of(i * tile, tile), tile)
+        attended = att[rows, :]
+        inverse = 1.0 / jnp.sqrt(jnp.mean(attended * attended, axis=1, keepdims=True) + NORM_EPS)
+        normed = attended * inverse
+        upstream = cot_ref[rows, :].astype(jnp.float32) * (1.0 / token_total)
+        inner = jnp.mean(upstream * normed, axis=1, keepdims=True)
+        outg[rows, :] = ((upstream - normed * inner) * inverse).astype(outg.dtype)
+        return carry
+
+    lax.fori_loop(0, tok_rows // tile, norm_step, 0)
+
+    def send_share(kv, back):
+        cut = pl.ds(kv * HEAD, HEAD)
+        peer = {"cp": jnp.maximum(p.c - back, 0), "fs": p.f}
+        number = kv * WIN + back - 1
+        return remote(
+            share.at[back - 1, :, cut], got.at[back - 1, :, cut], send.at[number], recv.at[number], peer
+        )
+
+    for kv in range(KV_HEADS):
+        total = None
+        for h in range(kv * GROUP, (kv + 1) * GROUP):
+            term = lax.dot_general(
+                outg[:, h * HEAD : (h + 1) * HEAD],
+                probs[h],
+                (((0,), (0,)), ((), ())),
+                preferred_element_type=jnp.float32,
+            )
+            total = term if total is None else total + term
+        cut = slice(kv * HEAD, (kv + 1) * HEAD)
+        for back in range(WIN, -1, -1):
+            first = (WIN - back) * tok_rows
+            block = total[:, first : first + tok_rows].T
+            if back == 0:
+                own[:, cut] = block
+            else:
+                share[back - 1, :, cut] = block.astype(share.dtype)
+
+                @pl.when(p.c >= back)
+                def _():
+                    send_share(kv, back).start()
+
+    def spread(f, kv, number, peer):
+        piece = all_ref.at[f, :, pl.ds(kv * HEAD, HEAD)]
+        return remote(piece, piece, gsend.at[number], grecv.at[number], peer)
+
+    for kv in range(KV_HEADS):
+        base = kv * (2 * far - 1)
+        cut = slice(kv * HEAD, (kv + 1) * HEAD)
+        for back in range(1, WIN + 1):
+
+            @pl.when(p.c + back < n)
+            def _():
+                send_share(kv, back).wait_recv()
+
+        total = own[:, cut]
+        for back in range(1, WIN + 1):
+            total = total + got[back - 1, :, cut].astype(jnp.float32)
+        all_ref[p.f, :, cut] = total.astype(all_ref.dtype)
+        for e in range(1, far):
+            pending.append(spread(p.f, kv, base + e - 1, p.across(e)))
+            pending[-1].start()
+        pending.append(spread(p.f, kv, base + far - 1, p.twin))
+        pending[-1].start()
+    for kv in range(KV_HEADS):
+        base = kv * (2 * far - 1)
+        for e in range(1, far):
+            g = (p.f + m - 2 * e) % m
+            spread(g, kv, base + e - 1, p.twin).wait_recv()
+            pending.append(spread(g, kv, base + far - 1 + e, p.twin))
+            pending[-1].start()
+    for kv in range(KV_HEADS):
+        base = kv * (2 * far - 1)
+        for e in range(far):
+            g = (p.twin_f + m - 2 * e) % m
+            spread(g, kv, base + far - 1 + e, p.twin).wait_recv()
     for k in range(strips):
         for e in range(1, m):
             g = (p.f + m - e) % m
             number = k * (m - 1) + e - 1
             remote(
-                cols_ref.at[k, g], cols_ref.at[k, g], send.at[number], recv.at[number], others[0]
+                cols_ref.at[k, g], cols_ref.at[k, g], csend.at[number], crecv.at[number], others[0]
             ).wait_recv()
     for copy in pending:
         copy.wait_send()
-
-
-def exchange_columns(values, embeds, strips, wide, n, m):
+    for kv in range(KV_HEADS):
+        for back in range(1, WIN + 1):
+
+            @pl.when(p.c >= back)
+            def _():
+                send_share(kv, back).wait_send()
+
+
+def attend(queries, cots, doc, listed, key_window, values, embeds, strips, wide, n, m):
     tok_rows, width = values.shape
+    span_rows = (WIN + 1) * tok_rows
+    heads = KV_HEADS * GROUP
     copies = strips * (m - 1)
+    gathers = KV_HEADS * (m - 1)
+    dma = pltpu.SemaphoreType.DMA
+    low = jnp.bfloat16
     return pl.pallas_call(
-        lambda *refs: column_kernel(n, m, *refs),
+        lambda *refs: attend_kernel(n, m, tok_rows * n * m, *refs),
         out_shape=(
-            jax.ShapeDtypeStruct(((WIN + 1) * tok_rows, width), values.dtype),
             jax.ShapeDtypeStruct((strips, m, tok_rows, wide), embeds.dtype),
+            jax.ShapeDtypeStruct((m, tok_rows, width), low),
         ),
-        in_specs=[pl.BlockSpec(memory_space=pltpu.VMEM)] * 2,
+        in_specs=[pl.BlockSpec(memory_space=pltpu.VMEM)] * 7,
         out_specs=(pl.BlockSpec(memory_space=pltpu.VMEM),) * 2,
         scratch_shapes=[
-            pltpu.SemaphoreType.DMA((copies,)),
-            pltpu.SemaphoreType.DMA((copies,)),
-            pltpu.SemaphoreType.DMA((WIN,)),
-            pltpu.SemaphoreType.DMA((WIN,)),
+            pltpu.VMEM((span_rows, width), low),
+            pltpu.VMEM((tok_rows, span_rows), jnp.float32),
+            pltpu.VMEM((heads, tok_rows, span_rows), low),
+            pltpu.VMEM((tok_rows, heads * HEAD), jnp.float32),
+            pltpu.VMEM((tok_rows, heads * HEAD), low),
+            pltpu.VMEM((tok_rows, width), jnp.float32),
+            pltpu.VMEM((WIN, tok_rows, width), low),
+            pltpu.VMEM((WIN, tok_rows, width), low),
+            dma((copies,)),
+            dma((copies,)),
+            dma((WIN,)),
+            dma((WIN,)),
+            dma((KV_HEADS * WIN,)),
+            dma((KV_HEADS * WIN,)),
+            dma((gathers,)),
+            dma((gathers,)),
         ],
         compiler_params=pltpu.CompilerParams(
             collective_id=2, has_side_effects=True, vmem_limit_bytes=VMEM_LIMIT
         ),
-        name="exchange_columns",
-    )(values, embeds)
-
-
-CHUNKS = 2
-
-
-def return_kernel(n, m, own_ref, share_ref, all_ref, got, send, recv, gsend, grecv):
-    p = Place(n, m)
-    tok_rows = own_ref.shape[0]
-    part = tok_rows // CHUNKS
-    far = m // 2
-    around = []
-    for back in range(1, WIN + 1):
-        around.append({"cp": (p.c + back) % n, "fs": p.f})
-        around.append({"cp": (p.c + n - back) % n, "fs": p.f})
-    signal_and_wait(around + p.acrosses() + [p.twin])
-
-    def share(chunk, back):
-        rows = pl.ds(chunk * part, part)
-        peer = {"cp": jnp.maximum(p.c - back, 0), "fs": p.f}
-        number = chunk * WIN + back - 1
-        return remote(
-            share_ref.at[back - 1, rows], got.at[back - 1, rows], send.at[number], recv.at[number], peer
-        )
-
-    for chunk in range(CHUNKS):
-        for back in (4, 3, 2, 1):
-
-            @pl.when(p.c >= back)
-            def _():
-                share(chunk, back).start()
-
-    for back in range(1, WIN + 1):
-
-        @pl.when(p.c + back >= n)
-        def _():
-            got[back - 1] = jnp.zeros(got.shape[1:], got.dtype)
-
-    def spread(f, chunk, number, peer):
-        piece = all_ref.at[f, pl.ds(chunk * part, part)]
-        return remote(piece, piece, gsend.at[number], grecv.at[number], peer)
-
-    pending = []
-    for chunk in range(CHUNKS):
-        base = chunk * (2 * far - 1)
-        rows = pl.ds(chunk * part, part)
-        for back in range(1, WIN + 1):
-
-            @pl.when(p.c + back < n)
-            def _():
-                share(chunk, back).wait_recv()
-
-        total = own_ref[rows, :]
-        for back in range(1, WIN + 1):
-            total = total + got[back - 1, rows, :].astype(jnp.float32)
-        all_ref[p.f, rows, :] = total.astype(all_ref.dtype)
-        for e in range(1, far):
-            pending.append(spread(p.f, chunk, base + e - 1, p.across(e)))
-            pending[-1].start()
-        pending.append(spread(p.f, chunk, base + far - 1, p.twin))
-        pending[-1].start()
-    for chunk in range(CHUNKS):
-        base = chunk * (2 * far - 1)
-        for e in range(1, far):
-            g = (p.f + m - 2 * e) % m
-            spread(g, chunk, base + e - 1, p.twin).wait_recv()
-            pending.append(spread(g, chunk, base + far - 1 + e, p.twin))
-            pending[-1].start()
-    for chunk in range(CHUNKS):
-        base = chunk * (2 * far - 1)
-        for e in range(far):
-            g = (p.twin_f + m - 2 * e) % m
-            spread(g, chunk, base + far - 1 + e, p.twin).wait_recv()
-    for copy in pending:
-        copy.wait_send()
-    for chunk in range(CHUNKS):
-        for back in range(1, WIN + 1):
-
-            @pl.when(p.c >= back)
-            def _():
-                share(chunk, back).wait_send()
-
-
-def return_shares(own, shares, n, m):
-    tok_rows, width = own.shape
-    gathers = CHUNKS * (m - 1)
-    return pl.pallas_call(
-        lambda *refs: return_kernel(n, m, *refs),
-        out_shape=jax.ShapeDtypeStruct((m, tok_rows, width), jnp.bfloat16),
-        in_specs=[pl.BlockSpec(memory_space=pltpu.VMEM)] * 2,
-        out_specs=pl.BlockSpec(memory_space=pltpu.VMEM),
-        scratch_shapes=[
-            pltpu.VMEM(shares.shape, shares.dtype),
-            pltpu.SemaphoreType.DMA((CHUNKS * WIN,)),
-            pltpu.SemaphoreType.DMA((CHUNKS * WIN,)),
-            pltpu.SemaphoreType.DMA((gathers,)),
-            pltpu.SemaphoreType.DMA((gathers,)),
-        ],
-        compiler_params=pltpu.CompilerParams(
-            collective_id=3, has_side_effects=True, vmem_limit_bytes=VMEM_LIMIT
-        ),
-        name="return_shares",
-    )(own, shares)
+        name="attend",
+    )(queries, cots, doc, listed, key_window, values, embeds)
 
 
 def reduce_kernel(n, m, part_ref, out_ref, mate_got, sums, got, msend, mrecv, send, recv):
@@ -467,69 +544,10 @@
     )(parts)
 
 
-def visible(doc_rows, need_row, block_id, tok_rows):
+def listed_keys(need_row, block_id, tok_rows):
     span_rows = (WIN + 1) * tok_rows
-    query_pos = block_id * tok_rows + jnp.arange(tok_rows, dtype=jnp.int32)
-    key_pos = (block_id - WIN) * tok_rows + jnp.arange(span_rows, dtype=jnp.int32)
     key_block = block_id - WIN + jnp.arange(span_rows, dtype=jnp.int32) // tok_rows
-    listed = jnp.any(need_row[None, :] == key_block[:, None], axis=1)
-    return (
-        (key_pos[None, :] >= doc_rows[:, None])
-        & (key_pos[None, :] <= query_pos[:, None])
-        & listed[None, :]
-    )
-
-
-def block_attention(query_rows, key_window, value_window, allowed):
-    tok_rows = query_rows.shape[0]
-    scaling = 1.0 / math.sqrt(HEAD)
-    query_split = query_rows.reshape(tok_rows, KV_HEADS, GROUP, HEAD)
-    prob_list = []
-    out_list = []
-    for kv_head in range(KV_HEADS):
-        key_part = key_window[:, kv_head * HEAD : (kv_head + 1) * HEAD]
-        value_part = value_window[:, kv_head * HEAD : (kv_head + 1) * HEAD]
-        scores = (
-            jnp.einsum(
-                "tgh,sh->gts", query_split[:, kv_head], key_part, preferred_element_type=jnp.float32
-            )
-            * scaling
-        )
-        scores = jnp.where(allowed[None], scores, -jnp.inf)
-        largest = jnp.max(scores, axis=-1, keepdims=True)
-        weights = jnp.exp(scores - largest)
-        probs_low = (weights / jnp.sum(weights, axis=-1, keepdims=True)).astype(jnp.bfloat16)
-        prob_list.append(probs_low)
-        out_list.append(
-            jnp.einsum("gts,sh->tgh", probs_low, value_part, preferred_element_type=jnp.float32)
-        )
-    attended = jnp.stack(out_list, axis=1).reshape(tok_rows, KV_HEADS * GROUP * HEAD)
-    return (prob_list, attended)
-
-
-def norm_backward(attended, cot_rows, token_total):
-    square_mean = jnp.mean(attended * attended, axis=-1, keepdims=True) + NORM_EPS
-    root_scale = jnp.sqrt(square_mean)
-    normed = attended / root_scale
-    upstream = cot_rows.astype(jnp.float32) / token_total
-    inner = jnp.mean(upstream * normed, axis=-1, keepdims=True)
-    return ((upstream - normed * inner) / root_scale).astype(jnp.bfloat16)
-
-
-def window_grads(prob_list, out_grad):
-    tok_rows = out_grad.shape[0]
-    grad_split = out_grad.reshape(tok_rows, KV_HEADS, GROUP, HEAD)
-    head_parts = []
-    for kv_head in range(KV_HEADS):
-        head_parts.append(
-            jnp.einsum(
-                "gts,tgh->sh",
-                prob_list[kv_head],
-                grad_split[:, kv_head],
-                preferred_element_type=jnp.float32,
-            )
-        )
-    return jnp.concatenate(head_parts, axis=1)
+    return jnp.any(need_row[None, :] == key_block[:, None], axis=1).astype(jnp.int32)[None, :]
 
 
 def on_device(
@@ -548,7 +566,6 @@
     tok_rows = tokens_here.shape[0]
     kv_width = key_heads.shape[2]
     block_id = lax.axis_index("cp")
-    token_total = tok_rows * lax.axis_size("cp") * lax.axis_size("fs")
     n, m = lax.axis_size("cp"), lax.axis_size("fs")
     own_rows = y_weight.shape[0]
     full_weight, key_window = gather_weight(y_weight, key_heads[0], n, m)
@@ -564,13 +581,19 @@
             .transpose(0, 2, 1, 3)
             .reshape(tok_rows, n * m * own_rows)
         )
-    value_window, group_cols = exchange_columns(values, sent_cols, strips, wide, n, m)
-    allowed = visible(doc_start[0], need_ids[0, 0], block_id, tok_rows)
-    prob_list, attended = block_attention(queries[0], key_window, value_window, allowed)
-    out_grad = norm_backward(attended, cotangent[0], token_total)
-    shares = window_grads(prob_list, out_grad).reshape(WIN + 1, tok_rows, kv_width)
-    sent_shares = shares[:WIN][::-1].astype(jnp.bfloat16)
-    group_grads = return_shares(shares[WIN], sent_shares, n, m)
+    group_cols, group_grads = attend(
+        queries[0],
+        cotangent[0],
+        doc_start[0][:, None],
+        listed_keys(need_ids[0, 0], block_id, tok_rows),
+        key_window,
+        values,
+        sent_cols,
+        strips,
+        wide,
+        n,
+        m,
+    )
     parts = jnp.einsum(
         "stw,te->swe",
         group_cols.reshape(strips, m * tok_rows, wide),

time: 232 us -> 161 us (0.69)
  matrix products: 37.8 us -> 8.98 us
  other arithmetic: 29.9 us -> 2.13 us
  local copies, waits for them, and re-layouts: 14.7 us -> 1.44 us
    sub x4 -> x0, matrix products: 20.9 us -> none  [block_attention(): weights = jnp.exp(scores - largest)]
    convert_element_type x5 -> x1, other arithmetic: 18 us -> 0.01 us  [listed_keys(): jnp.any(need_row[None, :] == key_block[:, None], axis=1).astype(jnp.int32)]
    dot_general x8 -> x0, matrix products: 11.4 us -> none  [the longest x4 8.02 us: block_attention(): jnp.einsum('gts,sh->tgh', probs_low, value_part, preferred_element_type=j...]
    unnamed x39 -> x12, local copies, waits for them, and re-layouts: 7.61 us -> 0.04 us
    pallas_call x1, Pallas kernels: 28 us -> 21.7 us  [reduce_parts(): pl.pallas_call(lambda *refs: reduce_kernel(n, m, *refs), out_shape=jax.Sh...]
    pallas_call x2 -> x1, Pallas kernels: 82.4 us -> 88.5 us  [attend(): pl.pallas_call(lambda *refs: attend_kernel(n, m, tok_rows * n * m, *refs)...]
    reduce_sum x2 -> x0, other arithmetic: 3.96 us -> none  [the longest x1 2.39 us: norm_backward(): inner = jnp.mean(upstream * normed, axis=-1, keepdims=True)]
    reshape x1 -> x0, local copies, waits for them, and re-layouts: 3.14 us -> none  [block_attention(): jnp.stack(out_list, axis=1).reshape(tok_rows, KV_HEADS * GROUP * HEAD)]
where the time goes in v2:
time: 161 us
  Pallas kernels  148 us (92%)
  matrix products  8.98 us (6%)
  other arithmetic  2.13 us (1%)
    pallas_call x1, Pallas kernels, attend(): pl.pallas_call(lambda *refs: attend_kernel(n, m, tok_rows * n * m, *refs)...  88.5 us
    pallas_call x1, Pallas kernels, gather_weight(): pl.pallas_call(lambda *refs: weight_kernel(n, m, *refs), out_shape=(jax.S...  37.3 us
    pallas_call x1, Pallas kernels, reduce_parts(): pl.pallas_call(lambda *refs: reduce_kernel(n, m, *refs), out_shape=jax.Sh...  21.7 us
    dot_general x1, matrix products, on_device(): jnp.dot(tokens_here, full_weight, preferred_element_type=jnp.float32)  4.78 us
    dot_general x1, matrix products, on_device(): jnp.einsum('stw,te->swe', group_cols.reshape(strips, m * tok_rows, wide),...  4.2 us

profile of v2, /device:TPU:0, one launch (start us, length us, event | category | flops | bytes accessed | tf_op | source)
XLA Modules:
  0.0 160.8 jit_solution(1532522946295350335)
XLA Ops:
  0.6 37.3 %gather_weight.1 = (bf16[4096,512]{1,0:T(8,128)(2,1)}, bf16[1280,512]{1,0:T(8,128)(2,1)}) custom-call(bf16[128,512]{1,0:T(8,128)(2,1)} %refs_0_.1, bf16[256,512]{1,0:T(8,128)(2,1)} %bitcast.21), custom_call_target="tpu_custom_call" | custom-call | tf_op jit(solution)/shard_map/gather_weight/pallas_call | solution.py:234
  37.9 0.0 copy-start.4
  37.9 0.0 copy-start.5
  38.0 4.8 %fusion.refs_5_ = bf16[256,512]{1,0:T(8,128)(2,1)} fusion(bf16[4096,512]{1,0:T(8,128)(2,1)} %get-tuple-element.9, bf16[1,256,4096]{2,1,0:T(8,128)(2,1)} %param.10), kind=kOutput, calls=%fused_computation.2 | convolution fusion | flops 1073872896 | bytes 6553600 | tf_op jit(solution)/shard_map/dot_general | solution.py:572
  42.7 0.0 copy-done.4
  42.7 0.8 copy.20.refs_2_
  43.5 0.0 copy-done.5
  43.5 0.1 compare_reduce_fusion
  43.6 0.6 reshape.34.refs_3_
  44.2 88.5 %attend.1 = (bf16[8,4,256,128]{3,2,1,0:T(8,128)(2,1)}, bf16[4,256,512]{2,1,0:T(8,128)(2,1)}) custom-call(bf16[256,2048]{1,0:T(8,128)(2,1)} %bitcast.19, bf16[256,2048]{1,0:T(8,128)(2,1)} %bitcast.20, s32[256,1]{1,0:T(8,128)} %copy.20.refs_2_, s32[1,1280]{1,0:T(1,128)} %reshape.34.refs_3_, bf16[1280,512]{1,0:T(8,128)(2,1)} %get-tuple-element.8.refs_4_, ...), custom_call_target="tpu_custom_call" | custom-call | tf_op jit(solution)/shard_map/attend/pallas_call | solution.py:464
  132.8 0.0 copy-start
  132.8 0.0 copy-start.1
  132.8 0.0 copy-start.2
  132.8 0.0 copy-start.3
  132.8 4.2 %bitcast_convert_fusion.refs_0_ = bf16[8,128,512]{2,1,0:T(8,128)(2,1)} fusion(bf16[8,4,256,128]{3,2,1,0:T(8,128)(2,1)} %get-tuple-element.10, bf16[4,256,512]{2,1,0:T(8,128)(2,1)} %get-tuple-element.11), kind=kOutput, calls=%fused_computation | convolution fusion | flops 1074266112 | bytes 4194304 | tf_op jit(solution)/shard_map/stw,te->swe/dot_general | solution.py:597
  137.0 21.7 %reduce_parts.1 = f32[128,512]{1,0:T(8,128)} custom-call(bf16[8,128,512]{2,1,0:T(8,128)(2,1)} %bitcast_convert_fusion.refs_0_), custom_call_target="tpu_custom_call" | custom-call | tf_op jit(solution)/shard_map/reduce_parts/pallas_call | solution.py:533
  158.8 0.0 copy-done
  158.8 0.0 copy-done.1
  158.8 0.0 copy-done.2
  158.8 0.0 copy-done.3
  158.8 2.0 %add_convert_fusion = (bf16[128,512]{1,0:T(8,128)(2,1)}, f32[128,512]{1,0:T(8,128)}, f32[128,512]{1,0:T(8,128)}, f32[128,512]{1,0:T(8,128)}) fusion(f32[128,512]{1,0:T(8,128)S(1)} %copy-done.1, f32[128,512]{1,0:T(8,128)S(1)} %copy-done.2, bf16[128,512]{1,0:T(8,128)(2,1)S(1)} %copy-done, f32[128,512]{1,0:T(8,128)} %reduce_parts.1, f32[128,512]{1,0:T(8,128)S(1)} %copy-done.3), kind=kLoop, calls=%fused_computation.6 | loop fusion | flops 1179648 | bytes 2097152 | tf_op jit(solution)/shard_map/convert_element_type | solution.py:609
  (2 shorter events, 0.0 us)
Async XLA Ops:
  37.9 4.8 %copy-start.4 = (s32[1,256]{1,0:T(1,128)S(1)}, s32[1,256]{1,0:T(1,128)}, u32[]{:S(2)}) copy-start(s32[1,256]{1,0:T(1,128)} %param.14) | copy-start | bytes 3076
  37.9 5.6 %copy-start.5 = (s32[1,1,5]{2,1,0:T(1,128)S(1)}, s32[1,1,5]{2,1,0:T(1,128)}, u32[]{:S(2)}) copy-start(s32[1,1,5]{2,1,0:T(1,128)} %param.15) | copy-start | bytes 64
  132.8 26.0 %copy-start = (bf16[128,512]{1,0:T(8,128)(2,1)S(1)}, bf16[128,512]{1,0:T(8,128)(2,1)}, u32[]{:S(2)}) copy-start(bf16[128,512]{1,0:T(8,128)(2,1)} %refs_0_.1) | copy-start | bytes 393220
  132.8 26.0 %copy-start.1 = (f32[128,512]{1,0:T(8,128)S(1)}, f32[128,512]{1,0:T(8,128)}, u32[]{:S(2)}) copy-start(f32[128,512]{1,0:T(8,128)} %param.18) | copy-start | bytes 786436
  132.8 26.0 %copy-start.2 = (f32[128,512]{1,0:T(8,128)S(1)}, f32[128,512]{1,0:T(8,128)}, u32[]{:S(2)}) copy-start(f32[128,512]{1,0:T(8,128)} %param.17) | copy-start | bytes 786436
  132.8 26.0 %copy-start.3 = (f32[128,512]{1,0:T(8,128)S(1)}, f32[128,512]{1,0:T(8,128)}, u32[]{:S(2)}) copy-start(f32[128,512]{1,0:T(8,128)} %param.19) | copy-start | bytes 786436

commit v3 on v2

--- a/solution.py
+++ b/solution.py
@@ -345,9 +345,9 @@
         probs[h] = (weights * (1.0 / jnp.sum(weights, axis=1, keepdims=True))).astype(probs.dtype)
         return carry
 
-    lax.fori_loop(0, heads * 5 // 8, prob_step, 0)
+    lax.fori_loop(0, heads * 5 // 8, prob_step, 0, unroll=2)
     window.relay()
-    lax.fori_loop(heads * 5 // 8, heads, prob_step, 0)
+    lax.fori_loop(heads * 5 // 8, heads, prob_step, 0, unroll=2)
     window.end()
 
     def out_step(h, carry):
@@ -356,7 +356,7 @@
         )
         return carry
 
-    lax.fori_loop(0, heads, out_step, 0)
+    lax.fori_loop(0, heads, out_step, 0, unroll=4)
     tile = 32
 
     def norm_step(i, carry):

time: 161 us -> 160 us (level)
  no operation moved by 1% of the time
where the time goes in v3:
time: 160 us
  Pallas kernels  147 us (92%)
  matrix products  8.98 us (6%)
  other arithmetic  2.13 us (1%)
    pallas_call x1, Pallas kernels, attend(): pl.pallas_call(lambda *refs: attend_kernel(n, m, tok_rows * n * m, *refs)...  87.4 us
    pallas_call x1, Pallas kernels, gather_weight(): pl.pallas_call(lambda *refs: weight_kernel(n, m, *refs), out_shape=(jax.S...  37.3 us
    pallas_call x1, Pallas kernels, reduce_parts(): pl.pallas_call(lambda *refs: reduce_kernel(n, m, *refs), out_shape=jax.Sh...  22.1 us
    dot_general x1, matrix products, on_device(): jnp.dot(tokens_here, full_weight, preferred_element_type=jnp.float32)  4.78 us
    dot_general x1, matrix products, on_device(): jnp.einsum('stw,te->swe', group_cols.reshape(strips, m * tok_rows, wide),...  4.2 us

profile of v3, /device:TPU:0, one launch (start us, length us, event | category | flops | bytes accessed | tf_op | source)
XLA Modules:
  0.0 160.1 jit_solution(4921206393391742607)
XLA Ops:
  0.6 37.3 %gather_weight.1 = (bf16[4096,512]{1,0:T(8,128)(2,1)}, bf16[1280,512]{1,0:T(8,128)(2,1)}) custom-call(bf16[128,512]{1,0:T(8,128)(2,1)} %refs_0_.1, bf16[256,512]{1,0:T(8,128)(2,1)} %bitcast.21), custom_call_target="tpu_custom_call" | custom-call | tf_op jit(solution)/shard_map/gather_weight/pallas_call | solution.py:234
  37.9 0.0 copy-start.4
  37.9 0.0 copy-start.5
  38.0 4.8 %fusion.refs_5_ = bf16[256,512]{1,0:T(8,128)(2,1)} fusion(bf16[4096,512]{1,0:T(8,128)(2,1)} %get-tuple-element.9, bf16[1,256,4096]{2,1,0:T(8,128)(2,1)} %param.10), kind=kOutput, calls=%fused_computation.2 | convolution fusion | flops 1073872896 | bytes 6553600 | tf_op jit(solution)/shard_map/dot_general | solution.py:572
  42.7 0.0 copy-done.4
  42.7 0.8 copy.20.refs_2_
  43.5 0.0 copy-done.5
  43.5 0.1 compare_reduce_fusion
  43.6 0.6 reshape.34.refs_3_
  44.2 87.4 %attend.1 = (bf16[8,4,256,128]{3,2,1,0:T(8,128)(2,1)}, bf16[4,256,512]{2,1,0:T(8,128)(2,1)}) custom-call(bf16[256,2048]{1,0:T(8,128)(2,1)} %bitcast.19, bf16[256,2048]{1,0:T(8,128)(2,1)} %bitcast.20, s32[256,1]{1,0:T(8,128)} %copy.20.refs_2_, s32[1,1280]{1,0:T(1,128)} %reshape.34.refs_3_, bf16[1280,512]{1,0:T(8,128)(2,1)} %get-tuple-element.8.refs_4_, ...), custom_call_target="tpu_custom_call" | custom-call | tf_op jit(solution)/shard_map/attend/pallas_call | solution.py:464
  131.7 0.0 copy-start
  131.7 0.0 copy-start.1
  131.7 0.0 copy-start.2
  131.7 0.0 copy-start.3
  131.7 4.2 %bitcast_convert_fusion.refs_0_ = bf16[8,128,512]{2,1,0:T(8,128)(2,1)} fusion(bf16[8,4,256,128]{3,2,1,0:T(8,128)(2,1)} %get-tuple-element.10, bf16[4,256,512]{2,1,0:T(8,128)(2,1)} %get-tuple-element.11), kind=kOutput, calls=%fused_computation | convolution fusion | flops 1074266112 | bytes 4194304 | tf_op jit(solution)/shard_map/stw,te->swe/dot_general | solution.py:597
  135.9 22.1 %reduce_parts.1 = f32[128,512]{1,0:T(8,128)} custom-call(bf16[8,128,512]{2,1,0:T(8,128)(2,1)} %bitcast_convert_fusion.refs_0_), custom_call_target="tpu_custom_call" | custom-call | tf_op jit(solution)/shard_map/reduce_parts/pallas_call | solution.py:533
  158.0 0.0 copy-done
  158.0 0.0 copy-done.1
  158.0 0.0 copy-done.2
  158.0 0.0 copy-done.3
  158.0 2.0 %add_convert_fusion = (bf16[128,512]{1,0:T(8,128)(2,1)}, f32[128,512]{1,0:T(8,128)}, f32[128,512]{1,0:T(8,128)}, f32[128,512]{1,0:T(8,128)}) fusion(f32[128,512]{1,0:T(8,128)S(1)} %copy-done.1, f32[128,512]{1,0:T(8,128)S(1)} %copy-done.2, bf16[128,512]{1,0:T(8,128)(2,1)S(1)} %copy-done, f32[128,512]{1,0:T(8,128)} %reduce_parts.1, f32[128,512]{1,0:T(8,128)S(1)} %copy-done.3), kind=kLoop, calls=%fused_computation.6 | loop fusion | flops 1179648 | bytes 2097152 | tf_op jit(solution)/shard_map/convert_element_type | solution.py:609
  (2 shorter events, 0.0 us)
Async XLA Ops:
  37.9 4.8 %copy-start.4 = (s32[1,256]{1,0:T(1,128)S(1)}, s32[1,256]{1,0:T(1,128)}, u32[]{:S(2)}) copy-start(s32[1,256]{1,0:T(1,128)} %param.14) | copy-start | bytes 3076
  37.9 5.6 %copy-start.5 = (s32[1,1,5]{2,1,0:T(1,128)S(1)}, s32[1,1,5]{2,1,0:T(1,128)}, u32[]{:S(2)}) copy-start(s32[1,1,5]{2,1,0:T(1,128)} %param.15) | copy-start | bytes 64
  131.7 26.3 %copy-start = (bf16[128,512]{1,0:T(8,128)(2,1)S(1)}, bf16[128,512]{1,0:T(8,128)(2,1)}, u32[]{:S(2)}) copy-start(bf16[128,512]{1,0:T(8,128)(2,1)} %refs_0_.1) | copy-start | bytes 393220
  131.7 26.3 %copy-start.1 = (f32[128,512]{1,0:T(8,128)S(1)}, f32[128,512]{1,0:T(8,128)}, u32[]{:S(2)}) copy-start(f32[128,512]{1,0:T(8,128)} %param.18) | copy-start | bytes 786436
  131.7 26.3 %copy-start.2 = (f32[128,512]{1,0:T(8,128)S(1)}, f32[128,512]{1,0:T(8,128)}, u32[]{:S(2)}) copy-start(f32[128,512]{1,0:T(8,128)} %param.17) | copy-start | bytes 786436
  131.7 26.3 %copy-start.3 = (f32[128,512]{1,0:T(8,128)S(1)}, f32[128,512]{1,0:T(8,128)}, u32[]{:S(2)}) copy-start(f32[128,512]{1,0:T(8,128)} %param.19) | copy-start | bytes 786436
